TPU v7x, 32 devices: a whole 2x2x4 slice. The times are simulated.
32 devices in a mesh: tp: 4 (over z), ep: 8 (over y, x, core).
Axes of the slice: x: 2, y: 2, z: 4, core: 2. Of those that a mesh axis runs over, the one named last changes fastest.
Arguments:
- tokens: bfloat16 [3072, 2048], P('ep', 'tp'), may hold values from -6 to 6
- norm_gain: float32 [2048], replicated, may hold values from 0.25 to 1.75
- shared_gate: bfloat16 [2048, 2816], P('ep', 'tp'), may hold values from -0.125 to 0.125
- shared_up: bfloat16 [2048, 2816], P('ep', 'tp'), may hold values from -0.125 to 0.125
- shared_down: bfloat16 [2816, 2048], P('tp', 'ep'), may hold values from -0.15625 to 0.15625
- expert_gate: bfloat16 [4, 8, 704, 2048], P('tp', 'ep'), may hold values from -0.125 to 0.125
- expert_up: bfloat16 [4, 8, 704, 2048], P('tp', 'ep'), may hold values from -0.125 to 0.125
- expert_down: bfloat16 [16, 1408, 2048], P('ep', None, 'tp'), may hold values from -0.15625 to 0.15625
- chosen: int32 [16, 384], P('ep'), may hold values from 0 to 3071, as said below
- gates: float32 [16, 384], P('ep'), may hold values from 0.1 to 1
Outputs:
- mixed: bfloat16 [3072, 2048], P('ep', 'tp')
Inputs may be any that keep to these rules, and one draw needn't show every extreme that they name: Each row of chosen holds 384 different token indices in rising order. Of one row, at most 96 lie among the 384 tokens of one index of ep (tokens s * 384 to (s + 1) * 384 - 1), and in every row exactly 96 lie among those of some index.
All inputs are finite; a program needn't handle non-finite values.
Results may differ from a plain program's by a relative error of at most 0.012.
Values may be sent and summed in bfloat16 or wider, within the bound.
A program may use at most 64 MiB of HBM per device.

v0:
```python
import functools

import jax
import jax.numpy as jnp
from jax import lax
from jax.experimental import pallas as pl
from jax.experimental.pallas import tpu as pltpu
from jax.sharding import PartitionSpec as P

norm_eps = 1e-06
MESH = pl.DeviceIdType.MESH


def flip(index, mask):
    bit = 1
    result = index
    while bit <= mask:
        if mask & bit:
            result = result + bit - 2 * bit * ((index // bit) % 2)
        bit *= 2
    return result


def bits_below(count):
    return [1 << i for i in range(count.bit_length() - 1)]


def half_orders(count):
    bits = bits_below(count)
    upper = bits[1:]
    return [upper + bits[:1], upper[::-1] + bits[:1]]


def later_hops(mask, order):
    last = max([i for i, b in enumerate(order) if mask & b], default=-1)
    return order[last + 1 :]


def masks_by_level(count):
    return sorted(range(1, count), key=lambda m: (bin(m).count("1"), -m))


def levels(count):
    found = {}
    for m in masks_by_level(count):
        found.setdefault(bin(m).count("1"), []).append(m)
    return [found[k] for k in sorted(found)]


def gather_kernel(
    n_tp,
    n_ep,
    tok_ref,
    sg_ref,
    su_ref,
    sd_ref,
    chosen_ref,
    ids_ref,
    sg_out,
    su_out,
    sd_out,
    own_out,
    used_out,
    ids_out,
    tok_all,
    sel,
    total,
    ep_send,
    ep_recv,
    tp_send,
    tp_recv,
    disp_send,
    disp_recv,
    local_sem,
):
    tp = lax.axis_index("tp")
    ep = lax.axis_index("ep")
    n_exp, cap = chosen_ref.shape[0], chosen_ref.shape[1]
    n_tok, width = tok_ref.shape
    split = n_tp // n_exp
    slot = tp // split
    orders = half_orders(n_ep)
    high_masks = [k * split for k in range(1, n_exp)]
    tp_bits = bits_below(n_tp)
    tp_order = tp_bits[::-1]
    tp_partners = sorted(set(tp_bits) | set(high_masks))

    barrier = pltpu.get_barrier_semaphore()
    for b in bits_below(n_ep):
        pl.semaphore_signal(barrier, inc=1, device_id={"ep": flip(ep, b)}, device_id_type=MESH)
    for b in tp_partners:
        pl.semaphore_signal(barrier, inc=1, device_id={"tp": flip(tp, b)}, device_id_type=MESH)
    pl.semaphore_wait(barrier, len(bits_below(n_ep)) + len(tp_partners))

    def block_of(out, block, rows):
        if len(out.shape) == 3:
            return out.at[block, rows, :]
        cols = out.shape[1] // n_ep
        return out.at[rows, pl.ds(pl.multiple_of(block * cols, cols), cols)]

    def sources(w):
        return [tok_ref, sg_ref, su_ref, sd_ref, ids_ref][w]

    def halves(w):
        return (0, 1) if w < 4 else (0,)

    def own_piece(w, h):
        ref = sources(w)
        if w == 4:
            return ref
        half = ref.shape[0] // 2
        return ref.at[pl.ds(h * half, half), :]

    def piece(w, block, h):
        ref = sources(w)
        if w == 4:
            return ids_out.at[block]
        half = ref.shape[0] // 2
        if w == 0:
            return tok_all.at[block, pl.ds(h * half, half), :]
        return block_of([None, sg_out, su_out, sd_out][w], block, pl.ds(h * half, half))

    def ep_copy(w, h, mask, hop):
        return pltpu.make_async_remote_copy(
            src_ref=own_piece(w, h) if mask == 0 else piece(w, flip(ep, mask), h),
            dst_ref=piece(w, flip(ep, mask), h),
            send_sem=ep_send.at[w, h, mask | hop],
            recv_sem=ep_recv.at[w, h, mask | hop],
            device_id={"ep": flip(ep, hop)},
            device_id_type=MESH,
        )

    def ep_arrival(w, h, mask):
        order = orders[h]
        hop = [b for b in order if mask & b][-1]
        dst = piece(w, flip(ep, mask), h)
        return pltpu.make_async_remote_copy(
            src_ref=dst,
            dst_ref=dst,
            send_sem=ep_send.at[w, h, mask],
            recv_sem=ep_recv.at[w, h, mask],
            device_id={"ep": flip(ep, hop)},
            device_id_type=MESH,
        )

    def ep_start(w):
        for position in range(len(orders[0])):
            for h in halves(w):
                ep_copy(w, h, 0, orders[h][position]).start()

    def ep_level(w, masks):
        for mask in masks:
            for h in halves(w):
                ep_arrival(w, h, mask).wait_recv()
                for hop in later_hops(mask, orders[h]):
                    ep_copy(w, h, mask, hop).start()

    def columns(ref, block):
        return ref.at[:, pl.ds(pl.multiple_of(block * width, width), width)]

    def tp_copy(mask, hop):
        return pltpu.make_async_remote_copy(
            src_ref=tok_ref if mask == 0 else columns(own_out, flip(tp, mask)),
            dst_ref=columns(own_out, flip(tp, mask)),
            send_sem=tp_send.at[mask | hop],
            recv_sem=tp_recv.at[mask | hop],
            device_id={"tp": flip(tp, hop)},
            device_id_type=MESH,
        )

    def used_piece(mask, h):
        rows = pl.ds(h * (cap // 2), cap // 2)
        cols = pl.ds(pl.multiple_of(flip(tp, mask) * width, width), width)
        return used_out.at[rows, cols]

    def disp_copy(mask, hop, h):
        if mask == 0:
            src = sel.at[flip(tp, hop) // split, pl.ds(h * (cap // 2), cap // 2), :]
        else:
            src = used_piece(mask, h)
        return pltpu.make_async_remote_copy(
            src_ref=src,
            dst_ref=used_piece(mask, h),
            send_sem=disp_send.at[mask | hop, h],
            recv_sem=disp_recv.at[mask | hop, h],
            device_id={"tp": flip(tp, hop)},
            device_id_type=MESH,
        )

    def disp_arrival(mask, h):
        dst = used_piece(mask, h)
        pltpu.make_async_remote_copy(
            src_ref=dst,
            dst_ref=dst,
            send_sem=disp_send.at[mask, h],
            recv_sem=disp_recv.at[mask, h],
            device_id={"tp": flip(tp, mask)},
            device_id_type=MESH,
        ).wait_recv()

    def low_hops(mask):
        low = mask % split
        return [b for b in bits_below(split) if b > low]

    def local_copies():
        items = [(0, tok_ref, tok_all.at[ep]), (6, ids_ref, ids_out.at[ep]), (1, tok_ref, columns(own_out, tp))]
        pairs = ((sg_ref, sg_out), (su_ref, su_out), (sd_ref, sd_out))
        for i, (ref, out) in enumerate(pairs):
            items.append((2 + i, ref, block_of(out, ep, pl.ds(0, ref.shape[0]))))
        return [pltpu.make_async_copy(s, d, local_sem.at[i]) for i, s, d in items]

    ep_start(0)
    for hop in tp_order:
        tp_copy(0, hop).start()
    locals_started = local_copies()
    for copy in locals_started:
        copy.start()
    ep_levels = levels(n_ep)
    ep_level(0, ep_levels[0])
    for w in (1, 2, 3, 4):
        ep_start(w)
    for masks in ep_levels[1:]:
        ep_level(0, masks)
    locals_started[0].wait()

    for s in range(n_exp):
        total[...] = jnp.zeros_like(total)

        def add_source(e, carry):
            ids = lax.broadcasted_iota(jnp.int32, (cap, n_tok), 1) + e * n_tok
            hits = jnp.where(chosen_ref[s] == ids, 1.0, 0.0).astype(jnp.bfloat16)
            total[...] += jnp.dot(hits, tok_all[e], preferred_element_type=jnp.float32)
            return carry

        lax.fori_loop(0, n_ep, add_source, 0)
        sel[s] = total[...].astype(jnp.bfloat16)

    for hop in high_masks + low_hops(0):
        for h in (0, 1):
            disp_copy(0, hop, h).start()
    own_used = pltpu.make_async_copy(sel.at[slot], columns(used_out, tp), local_sem.at[5])
    own_used.start()

    for w in (1, 2, 3, 4):
        ep_level(w, ep_levels[0])
    for mask in high_masks:
        for h in (0, 1):
            disp_arrival(mask, h)
            for hop in low_hops(mask):
                disp_copy(mask, hop, h).start()
    tp_seen = []
    for mask in sorted(range(1, n_tp), key=lambda m: [tp_order.index(b) for b in tp_order if m & b][-1]):
        last = [b for b in tp_order if mask & b][-1]
        if last == tp_order[0]:
            disp_wait(columns(own_out, flip(tp, mask)), tp_send, tp_recv, mask, tp)
            tp_seen.append(mask)
            for hop in later_hops(mask, tp_order):
                tp_copy(mask, hop).start()
    for masks in ep_levels[1:]:
        for w in (1, 2, 3, 4):
            ep_level(w, masks)
    for mask in range(1, n_tp):
        if mask not in high_masks:
            for h in (0, 1):
                disp_arrival(mask, h)
                for hop in low_hops(mask):
                    disp_copy(mask, hop, h).start()
    for mask in sorted(range(1, n_tp), key=lambda m: [tp_order.index(b) for b in tp_order if m & b][-1]):
        if mask not in tp_seen:
            disp_wait(columns(own_out, flip(tp, mask)), tp_send, tp_recv, mask, tp)
            for hop in later_hops(mask, tp_order):
                tp_copy(mask, hop).start()

    for copy in locals_started[1:]:
        copy.wait()
    own_used.wait()
    for w in range(5):
        for h in halves(w):
            for mask in range(n_ep):
                for hop in later_hops(mask, orders[h]):
                    ep_copy(w, h, mask, hop).wait_send()
    for mask in range(n_tp):
        for hop in later_hops(mask, tp_order):
            tp_copy(mask, hop).wait_send()
    for mask in [0] + high_masks + [m for m in range(1, n_tp) if m not in high_masks]:
        hops = low_hops(mask)
        if mask == 0:
            hops = high_masks + hops
        for hop in hops:
            for h in (0, 1):
                disp_copy(mask, hop, h).wait_send()


def disp_wait(dst, send_sem, recv_sem, mask, tp):
    pltpu.make_async_remote_copy(
        src_ref=dst,
        dst_ref=dst,
        send_sem=send_sem.at[mask],
        recv_sem=recv_sem.at[mask],
        device_id={"tp": flip(tp, mask)},
        device_id_type=MESH,
    ).wait_recv()


def upfront(n_tp, n_ep, tokens, shared_gate, shared_up, shared_down, chosen):
    n_tok, width = tokens.shape
    n_exp, cap = chosen.shape
    vmem = pl.BlockSpec(memory_space=pltpu.VMEM)
    hbm = pl.BlockSpec(memory_space=pl.ANY)
    bf16 = jnp.bfloat16

    def joined(weight):
        rows, cols = weight.shape
        if cols % 128 == 0:
            return jax.ShapeDtypeStruct((rows, n_ep * cols), bf16)
        return jax.ShapeDtypeStruct((n_ep, rows, cols), bf16)

    return pl.pallas_call(
        functools.partial(gather_kernel, n_tp, n_ep),
        out_shape=(
            joined(shared_gate),
            joined(shared_up),
            joined(shared_down),
            jax.ShapeDtypeStruct((n_tok, n_tp * width), bf16),
            jax.ShapeDtypeStruct((cap, n_tp * width), bf16),
            jax.ShapeDtypeStruct((n_ep, n_exp, cap), jnp.int32),
        ),
        in_specs=[vmem] + [hbm] * 3 + [vmem] * 2,
        out_specs=(hbm,) * 5 + (vmem,),
        scratch_shapes=[
            pltpu.VMEM((n_ep, n_tok, width), bf16),
            pltpu.VMEM((n_exp, cap, width), bf16),
            pltpu.VMEM((cap, width), jnp.float32),
            pltpu.SemaphoreType.DMA((5, 2, n_ep)),
            pltpu.SemaphoreType.DMA((5, 2, n_ep)),
            pltpu.SemaphoreType.DMA((n_tp,)),
            pltpu.SemaphoreType.DMA((n_tp,)),
            pltpu.SemaphoreType.DMA((n_tp, 2)),
            pltpu.SemaphoreType.DMA((n_tp, 2)),
            pltpu.SemaphoreType.DMA((7,)),
        ],
        compiler_params=pltpu.CompilerParams(
            collective_id=0, has_side_effects=True, vmem_limit_bytes=48 * 1024 * 1024
        ),
    )(tokens, shared_gate, shared_up, shared_down, chosen[:, :, None], chosen)


def flat_weight(weight):
    if weight.ndim == 2:
        return weight
    return jnp.moveaxis(weight, 0, 1).reshape(weight.shape[1], -1)


def normalise(rows, gain):
    widened = rows.astype(jnp.float32)
    inv_scale = lax.rsqrt(jnp.mean(widened * widened, axis=1, keepdims=True) + norm_eps)
    return (widened * inv_scale * gain).astype(jnp.bfloat16)


def finish_kernel(
    n_tp,
    n_ep,
    part_ref,
    normed_ref,
    sg_hbm,
    su_hbm,
    sd_hbm,
    down_hbm,
    gates_ref,
    place_ref,
    ids_ref,
    out_ref,
    sg_ref,
    su_ref,
    sd_ref,
    down_ref,
    hidden,
    acc,
    parts,
    parts_in,
    stage,
    back,
    load_sem,
    hid_send,
    hid_recv,
    sum_send,
    sum_recv,
    ret_send,
    ret_recv,
):
    tp = lax.axis_index("tp")
    ep = lax.axis_index("ep")
    n_tok, width = out_ref.shape
    n_exp = gates_ref.shape[0]
    split = n_tp // n_exp
    f32, bf16 = jnp.float32, jnp.bfloat16
    order = bits_below(n_tp)[::-1]
    half = part_ref.shape[0] // 2

    barrier = pltpu.get_barrier_semaphore()
    for mask in range(1, n_tp):
        pl.semaphore_signal(barrier, inc=1, device_id={"tp": flip(tp, mask)}, device_id_type=MESH)
    for mask in range(1, n_ep):
        pl.semaphore_signal(barrier, inc=1, device_id={"ep": flip(ep, mask)}, device_id_type=MESH)
    pl.semaphore_wait(barrier, n_tp + n_ep - 2)

    def hid_copy(mask, hop, h):
        rows = pl.ds(h * half, half)
        block = flip(tp, mask)
        return pltpu.make_async_remote_copy(
            src_ref=part_ref.at[rows, :] if mask == 0 else hidden.at[block, rows, :],
            dst_ref=hidden.at[block, rows, :],
            send_sem=hid_send.at[mask | hop, h],
            recv_sem=hid_recv.at[mask | hop, h],
            device_id={"tp": flip(tp, hop)},
            device_id_type=MESH,
        )

    def hid_arrived(mask, h):
        dst = hidden.at[flip(tp, mask), pl.ds(h * half, half), :]
        pltpu.make_async_remote_copy(
            src_ref=dst,
            dst_ref=dst,
            send_sem=hid_send.at[mask, h],
            recv_sem=hid_recv.at[mask, h],
            device_id={"tp": flip(tp, mask)},
            device_id_type=MESH,
        ).wait_recv()

    def sum_copy(mask):
        return pltpu.make_async_remote_copy(
            src_ref=parts.at[flip(tp, mask)],
            dst_ref=parts_in.at[mask],
            send_sem=sum_send.at[mask],
            recv_sem=sum_recv.at[mask],
            device_id={"tp": flip(tp, mask)},
            device_id_type=MESH,
        )

    def ret_copy(mask):
        return pltpu.make_async_remote_copy(
            src_ref=stage.at[flip(ep, mask)],
            dst_ref=back.at[ep],
            send_sem=ret_send.at[mask],
            recv_sem=ret_recv.at[mask],
            device_id={"ep": flip(ep, mask)},
            device_id_type=MESH,
        )

    def ret_arrived(mask):
        dst = back.at[flip(ep, mask)]
        pltpu.make_async_remote_copy(
            src_ref=dst,
            dst_ref=dst,
            send_sem=ret_send.at[mask],
            recv_sem=ret_recv.at[mask],
            device_id={"ep": flip(ep, mask)},
            device_id_type=MESH,
        ).wait_recv()

    for hop in order:
        for h in (0, 1):
            hid_copy(0, hop, h).start()
    pairs = ((sg_hbm, sg_ref), (su_hbm, su_ref), (sd_hbm, sd_ref), (down_hbm, down_ref))
    loads = [pltpu.make_async_copy(s, d, load_sem.at[i]) for i, (s, d) in enumerate(pairs)]
    for load in loads:
        load.start()

    for load in loads[:3]:
        load.wait()
    chunk = n_tok // 2

    def shared_rows(i, carry):
        rows = pl.ds(pl.multiple_of(i * chunk, chunk), chunk)
        x = normed_ref[rows, :]
        contract = (((1,), (1,)), ((), ()))
        gate = lax.dot_general(x, sg_ref[...], contract, preferred_element_type=f32)
        up = lax.dot_general(x, su_ref[...], contract, preferred_element_type=f32)
        mid = (jax.nn.silu(gate) * up).astype(bf16)
        for block in range(n_tp):
            cols = pl.ds(block * width, width)
            parts[block, rows, :] = jnp.dot(
                mid, sd_ref[:, cols], preferred_element_type=f32
            ).astype(bf16)
        return carry

    lax.fori_loop(0, 2, shared_rows, 0)
    loads[3].wait()

    acc[...] = jnp.zeros_like(acc)

    def add_block(mask):
        block = flip(tp, mask)
        value = part_ref[...] if mask == 0 else hidden[block]
        slot = block // split
        acc[slot] += lax.dot_general(
            value, down_ref[block], (((0,), (0,)), ((), ())), preferred_element_type=f32
        )

    arrivals = sorted(
        range(1, n_tp), key=lambda m: [order.index(b) for b in order if m & b][::-1]
    )
    tp_masks = list(range(1, n_tp))
    first_hop = [m for m in arrivals if m == order[0]]
    for mask in first_hop:
        for h in (0, 1):
            hid_arrived(mask, h)
            for hop in later_hops(mask, order):
                hid_copy(mask, hop, h).start()
    for mask in tp_masks:
        sum_copy(mask).start()
    add_block(0)
    for mask in first_hop:
        add_block(mask)
    for mask in arrivals:
        if mask in first_hop:
            continue
        for h in (0, 1):
            hid_arrived(mask, h)
            for hop in later_hops(mask, order):
                hid_copy(mask, hop, h).start()
        add_block(mask)

    slots = stage.shape[0] * stage.shape[2]
    for s in range(n_exp):
        weighted = (gates_ref[s] * acc[s]).astype(bf16)
        cap = weighted.shape[0]
        placer = lax.broadcasted_iota(jnp.int32, (slots, cap), 0) == place_ref[s]
        placer = jnp.where(placer, 1.0, 0.0).astype(bf16)
        placed = jnp.dot(placer, weighted, preferred_element_type=f32)
        stage[:, s] = placed.reshape(stage.shape[0], stage.shape[2], width).astype(bf16)
    ep_masks = sorted(range(1, n_ep), key=lambda m: -bin(m >> 1).count("1"))
    for mask in ep_masks:
        ret_copy(mask).start()
    back[ep] = stage[ep]

    ids = ids_ref[...]
    picker = lax.broadcasted_iota(jnp.int32, (n_tok, ids.shape[1]), 0) == ids
    picker = jnp.where(picker, 1.0, 0.0).astype(bf16)
    for mask in ep_masks:
        ret_arrived(mask)
    acc[0] = jnp.dot(picker, back[...].reshape(-1, width), preferred_element_type=f32)
    acc[0] += parts[tp].astype(f32)
    for mask in tp_masks:
        sum_copy(mask).wait_recv()
        acc[0] += parts_in[mask].astype(f32)
    out_ref[...] = acc[0].astype(bf16)

    for mask in [0] + arrivals:
        for hop in later_hops(mask, order):
            for h in (0, 1):
                hid_copy(mask, hop, h).wait_send()
    for mask in tp_masks:
        sum_copy(mask).wait_send()
    for mask in ep_masks:
        ret_copy(mask).wait_send()


def finish(n_tp, n_ep, slot_most, hidden, normed, sg, su, sd, down, gates, place, ids):
    n_tok = normed.shape[0]
    width = down.shape[2]
    n_exp, cap = gates.shape[:2]
    vmem = pl.BlockSpec(memory_space=pltpu.VMEM)
    hbm = pl.BlockSpec(memory_space=pl.ANY)
    bf16 = jnp.bfloat16
    dma = pltpu.SemaphoreType.DMA
    return pl.pallas_call(
        functools.partial(finish_kernel, n_tp, n_ep),
        out_shape=jax.ShapeDtypeStruct((n_tok, width), bf16),
        in_specs=[vmem, vmem, hbm, hbm, hbm, hbm, vmem, vmem, vmem],
        out_specs=vmem,
        scratch_shapes=[
            pltpu.VMEM(sg.shape, bf16),
            pltpu.VMEM(su.shape, bf16),
            pltpu.VMEM(sd.shape, bf16),
            pltpu.VMEM(down.shape, bf16),
            pltpu.VMEM((n_tp,) + hidden.shape, bf16),
            pltpu.VMEM((n_exp, cap, width), jnp.float32),
            pltpu.VMEM((n_tp, n_tok, width), bf16),
            pltpu.VMEM((n_tp, n_tok, width), bf16),
            pltpu.VMEM((n_ep, n_exp, slot_most, width), bf16),
            pltpu.VMEM((n_ep, n_exp, slot_most, width), bf16),
            dma((4,)),
            dma((n_tp, 2)),
            dma((n_tp, 2)),
            dma((n_tp,)),
            dma((n_tp,)),
            dma((n_ep,)),
            dma((n_ep,)),
        ],
        compiler_params=pltpu.CompilerParams(
            collective_id=1, has_side_effects=True, vmem_limit_bytes=56 * 1024 * 1024
        ),
    )(hidden, normed, sg, su, sd, down, gates, place, ids)


def on_device(
    tokens,
    norm_gain,
    shared_gate,
    shared_up,
    shared_down,
    expert_gate,
    expert_up,
    expert_down,
    chosen,
    gates,
):
    n_tp = lax.axis_size("tp")
    n_ep = lax.axis_size("ep")
    ep = lax.axis_index("ep")
    n_exp, cap = chosen.shape
    n_tok, width = tokens.shape
    f32 = jnp.float32

    sg, su, sd, own_rows, used_rows, all_chosen = upfront(
        n_tp, n_ep, tokens, shared_gate.T, shared_up.T, shared_down, chosen
    )
    sg, su, sd = flat_weight(sg), flat_weight(su), flat_weight(sd)
    all_chosen = all_chosen.reshape(-1, cap)

    slot_most = 2 * cap // n_ep
    positions = jnp.arange(cap, dtype=jnp.int32)
    sources = chosen // n_tok
    before = chosen[:, None, :] < (sources * n_tok)[:, :, None]
    run_start = jnp.sum(before.astype(jnp.int32), axis=2)
    slot_index = sources * slot_most + positions[None, :] - run_start
    first = jnp.sum((all_chosen < ep * n_tok).astype(jnp.int32), axis=1)
    stop = jnp.sum((all_chosen < (ep + 1) * n_tok).astype(jnp.int32), axis=1)
    slots = jnp.arange(slot_most, dtype=jnp.int32)
    wanted = first[:, None] + slots[None, :]
    wanted = jnp.where(wanted < stop[:, None], wanted, -1)
    own_ids = jnp.sum(
        jnp.where(
            wanted[:, :, None] == positions[None, None, :],
            (all_chosen - ep * n_tok + 1)[:, None, :],
            0,
        ),
        axis=2,
    ) - 1

    used = normalise(used_rows, norm_gain)
    gate_weight = expert_gate.reshape(expert_gate.shape[2], expert_gate.shape[3])
    up_weight = expert_up.reshape(expert_up.shape[2], expert_up.shape[3])
    gate_values = jnp.einsum("hd,rd->hr", gate_weight, used, preferred_element_type=f32)
    up_values = jnp.einsum("hd,rd->hr", up_weight, used, preferred_element_type=f32)
    part_hidden = (jax.nn.silu(gate_values) * up_values).astype(jnp.bfloat16)
    normed = normalise(own_rows, norm_gain)
    down = expert_down.reshape(n_tp, -1, width)
    return finish(
        n_tp,
        n_ep,
        slot_most,
        part_hidden,
        normed,
        sg,
        su,
        sd,
        down,
        gates[:, :, None],
        slot_index[:, None, :],
        own_ids.reshape(1, -1),
    )


def solution(mesh):
    return jax.shard_map(
        on_device,
        mesh=mesh,
        in_specs=(
            P("ep", "tp"),
            P(),
            P("ep", "tp"),
            P("ep", "tp"),
            P("tp", "ep"),
            P("tp", "ep", None, None),
            P("tp", "ep", None, None),
            P("ep", None, "tp"),
            P("ep", None),
            P("ep", None),
        ),
        out_specs=P("ep", "tp"),
        check_vma=False,
    )
```

profile of v0, /device:TPU:0, one launch (start us, length us, event | category | flops | bytes accessed | tf_op | source)
XLA Modules:
  0.0 155.8 jit_solution(2990141676249425929)
XLA Ops:
  0.0 1.0 copy.13.chosen_ref
  1.0 0.0 copy-start.2
  1.0 1.0 copy-done.2
  2.0 1.0 copy-done.3
  3.0 1.0 copy-done.4
  4.0 1.0 copy-done.5
  5.0 0.7 copy-done.6
  5.7 67.2 %shard_map.100 = (bf16[704,2048]{1,0:T(8,128)(2,1)}, bf16[704,2048]{1,0:T(8,128)(2,1)}, bf16[704,2048]{1,0:T(8,128)(2,1)}, bf16[384,2048]{1,0:T(8,128)(2,1)S(1)}...) custom-call(bf16[384,512]{1,0:T(8,128)(2,1)S(1)} %copy-done.2, bf16[704,256]{1,0:T(8,128)(2,1)S(1)} %bitcast.27, ...), custom_call_target="tpu_custom_call" | custom-call | tf_op jit(solution)/shard_map/pallas_call | solution.py:318
  72.8 0.7 fusion
  73.6 1.8 %fusion.10 = f32[704,384]{1,0:T(8,128)S(1)} fusion(bf16[1,1,704,2048]{3,2,1,0:T(8,128)(2,1)S(1)} %copy-done, bf16[384,2048]{1,0:T(8,128)(2,1)S(1)} %get-tuple-element.11, f32[2048]{0:T(1024)S(1)} %copy-done.8, f32[384]{0:T(512)S(1)} %add_rsqrt_fusion.1), kind=kOutput, calls=%fused_computation.16 | convolution fusion | flops 1110441984 | bytes 5547520 | tf_op jit(solution)/shard_map/hd,rd->hr/dot_general | solution.py:645
  75.3 0.0 copy-done.10
  75.4 2.6 %fusion.19.part_ref = bf16[704,384]{1,0:T(8,128)(2,1)} fusion(bf16[1,1,704,2048]{3,2,1,0:T(8,128)(2,1)S(1)} %copy-done.10, f32[704,384]{1,0:T(8,128)S(1)} %fusion.10, bf16[384,2048]{1,0:T(8,128)(2,1)S(1)} %get-tuple-element.11, f32[2048]{0:T(1024)S(1)} %copy-done.8, f32[384]{0:T(512)S(1)} %add_rsqrt_fusion.1), kind=kOutput, calls=%fused_computation.19 | convolution fusion | flops 1112064000 | bytes 6088192 | tf_op jit(solution)/shard_map/hd,rd->hr/dot_general | solution.py:646
  78.0 0.3 fusion.24
  78.3 0.1 add.78
  78.4 0.1 lt.48
  78.5 0.1 compare_select_fusion
  78.6 0.7 select_reduce_fusion
  79.3 0.7 sub.28.ids_ref
  80.0 3.0 %fusion.5.normed_ref = bf16[384,2048]{1,0:T(8,128)(2,1)} fusion(bf16[384,2048]{1,0:T(8,128)(2,1)} %copy-done.1, f32[384]{0:T(512)S(1)} %add_rsqrt_fusion, f32[2048]{0:T(1024)S(1)} %copy-done.8), kind=kLoop, calls=%fused_computation.9 | loop fusion | flops 3145728 | bytes 3155456 | tf_op jit(solution)/shard_map/convert_element_type | solution.py:357
  83.0 0.3 convert_reduce_fusion
  83.4 0.6 broadcast_in_dim.24.place_ref
  84.0 0.9 copy.14.gates_ref
  84.9 69.2 %shard_map.101 = bf16[384,512]{1,0:T(8,128)(2,1)} custom-call(bf16[704,384]{1,0:T(8,128)(2,1)} %fusion.19.part_ref, bf16[384,2048]{1,0:T(8,128)(2,1)} %fusion.5.normed_ref, bf16[704,2048]{1,0:T(8,128)(2,1)} %get-tuple-element.13.sg_hbm, bf16[704,2048]{1,0:T(8,128)(2,1)} %get-tuple-element.14.su_hbm, bf16[704,2048]{1,0:T(8,128)(2,1)} %get-tuple-element.15.sd_hbm, ...), custom_call_target="tpu_custom_call" | custom-call | tf_op jit(solution)/shard_map/pallas_call | solution.py:567
  154.1 1.8 %copy.16 = bf16[384,512]{1,0:T(8,128)(2,1)} copy(bf16[384,512]{1,0:T(8,128)(2,1)} %shard_map.101) | data formatting | bytes 786432
  (21 shorter events, 0.1 us)
Async XLA Ops:
  0.0 73.5 %copy-start = (bf16[1,1,704,2048]{3,2,1,0:T(8,128)(2,1)S(1)}, bf16[1,1,704,2048]{3,2,1,0:T(8,128)(2,1)}, u32[]{:S(2)}) copy-start(bf16[1,1,704,2048]{3,2,1,0:T(8,128)(2,1)} %param.15) | copy-start | bytes 8650756
  1.0 1.0 copy-start.2
  2.0 1.0 copy-start.3
  3.0 1.0 copy-start.4
  4.0 1.0 copy-start.5
  5.0 0.7 copy-start.6
  5.7 67.9 %copy-start.8 = (f32[2048]{0:T(1024)S(1)}, f32[2048]{0:T(1024)}, u32[]{:S(2)}) copy-start(f32[2048]{0:T(1024)} %param.11) | copy-start | bytes 24580
  72.8 2.5 %copy-start.1 = (bf16[384,2048]{1,0:T(8,128)(2,1)}, bf16[384,2048]{1,0:T(8,128)(2,1)S(1)}, u32[]{:S(2)}) copy-start(bf16[384,2048]{1,0:T(8,128)(2,1)S(1)} %get-tuple-element.12) | copy-start | bytes 4718596
  73.5 1.8 %copy-start.10 = (bf16[1,1,704,2048]{3,2,1,0:T(8,128)(2,1)S(1)}, bf16[1,1,704,2048]{3,2,1,0:T(8,128)(2,1)}, u32[]{:S(2)}) copy-start(bf16[1,1,704,2048]{3,2,1,0:T(8,128)(2,1)} %param.16) | copy-start | bytes 8650756
  78.0 5.0 %copy-start.7 = (s32[2,384]{1,0:T(2,128)S(1)}, s32[2,384]{1,0:T(2,128)}, u32[]{:S(2)}) copy-start(s32[2,384]{1,0:T(2,128)} %ids_ref.1) | copy-start | bytes 9220
  78.0 6.0 %copy-start.9 = (f32[2,384]{1,0:T(2,128)S(1)}, f32[2,384]{1,0:T(2,128)}, u32[]{:S(2)}) copy-start(f32[2,384]{1,0:T(2,128)} %param.19) | copy-start | bytes 9220
where the time goes:
time: 157 us; the launch traced here: 156 us
  Pallas kernels  136 us (87%)
  local copies, waits for them, and re-layouts  9.86 us (6%)
  other arithmetic  5.15 us (3%)
  matrix products  4.38 us (3%)
    pallas_call x1, Pallas kernels, finish(): pl.pallas_call(functools.partial(finish_kernel, n_tp, n_ep), out_shape=ja...  69.2 us
    pallas_call x1, Pallas kernels, upfront(): pl.pallas_call(functools.partial(gather_kernel, n_tp, n_ep), out_shape=(j...  67.2 us
    unnamed x23, local copies, waits for them, and re-layouts  6.46 us

commit v1 on v0

v1 whole, which is shorter than its diff:
```python
import functools

import jax
import jax.numpy as jnp
from jax import lax
from jax.experimental import pallas as pl
from jax.experimental.pallas import tpu as pltpu
from jax.sharding import PartitionSpec as P

norm_eps = 1e-06
MESH = pl.DeviceIdType.MESH


def flip(index, mask):
    bit = 1
    result = index
    while bit <= mask:
        if mask & bit:
            result = result + bit - 2 * bit * ((index // bit) % 2)
        bit *= 2
    return result


def bits_below(count):
    return [1 << i for i in range(count.bit_length() - 1)]


def half_orders(count):
    bits = bits_below(count)
    upper = bits[1:]
    return [upper + bits[:1], upper[::-1] + bits[:1]]


def later_hops(mask, order):
    last = max([i for i, b in enumerate(order) if mask & b], default=-1)
    return order[last + 1 :]


def masks_by_level(count):
    return sorted(range(1, count), key=lambda m: (bin(m).count("1"), -m))


def levels(count):
    found = {}
    for m in masks_by_level(count):
        found.setdefault(bin(m).count("1"), []).append(m)
    return [found[k] for k in sorted(found)]


def column_of(row, count):
    same = lax.broadcasted_iota(jnp.int32, (count, count), 0) == lax.broadcasted_iota(
        jnp.int32, (count, count), 1
    )
    return jnp.sum(jnp.where(same, row, 0.0), axis=1, keepdims=True)


def normalise(rows, gain):
    widened = rows.astype(jnp.float32)
    inv_scale = lax.rsqrt(jnp.mean(widened * widened, axis=1, keepdims=True) + norm_eps)
    return (widened * inv_scale * gain).astype(jnp.bfloat16)


def layer_kernel(
    n_tp,
    n_ep,
    slot_most,
    tok_hbm,
    gain_ref,
    sg_hbm,
    su_hbm,
    sd_hbm,
    eg_hbm,
    eu_hbm,
    down_hbm,
    chosen_ref,
    gates_ref,
    out_ref,
    tok_all,
    own_rows,
    used_rows,
    sel,
    sg_in,
    su_in,
    sd_in,
    eg_ref,
    eu_ref,
    down_ref,
    hidden,
    acc,
    parts,
    in_up,
    in_down,
    stage,
    back,
    picker,
    ids_out,
    ids_in,
    chosen_col,
    gates_col,
    place_row,
    ep_send,
    ep_recv,
    tp_send,
    tp_recv,
    disp_send,
    disp_recv,
    hid_send,
    hid_recv,
    up_send,
    up_recv,
    down_send,
    down_recv,
    ret_send,
    ret_recv,
    ids_send_sem,
    ids_recv_sem,
    local_sem,
    *flat,
):
    tp = lax.axis_index("tp")
    ep = lax.axis_index("ep")
    f32, bf16, i32 = jnp.float32, jnp.bfloat16, jnp.int32
    n_exp, cap = chosen_ref.shape
    n_tok, width = tok_hbm.shape
    n_hid = eg_ref.shape[0]
    slot_pad = back.shape[2]
    split = n_tp // n_exp
    slot = tp // split
    orders = half_orders(n_ep)
    high_masks = [k * split for k in range(1, n_exp)]
    tp_order = bits_below(n_tp)[::-1]
    ep_levels = levels(n_ep)
    cut = max(128, cap * 2 // 3 // 128 * 128)
    chunks = [(0, cut), (cut, cap - cut)]
    parts_of = range(len(chunks))

    own_loads = [
        (tok_hbm, tok_all.at[ep]),
        (sg_hbm, sg_in),
        (su_hbm, su_in),
        (sd_hbm, sd_in),
    ]

    def block_of(out, block, rows):
        if len(out.shape) == 3:
            return out.at[block, rows, :]
        cols = out.shape[1] // n_ep
        return out.at[rows, pl.ds(pl.multiple_of(block * cols, cols), cols)]

    def columns(ref, block):
        return ref.at[:, pl.ds(pl.multiple_of(block * width, width), width)]

    loads = []
    for i, (source, target) in enumerate(own_loads):
        if i > 0:
            target = block_of(target, ep, pl.ds(0, source.shape[0]))
        loads.append(pltpu.make_async_copy(source, target, local_sem.at[i]))
    loads.append(pltpu.make_async_copy(tok_hbm, columns(own_rows, tp), local_sem.at[4]))
    for i, (source, target) in enumerate(((eg_hbm, eg_ref), (eu_hbm, eu_ref), (down_hbm, down_ref))):
        loads.append(pltpu.make_async_copy(source, target, local_sem.at[5 + i]))
    for load in loads:
        load.start()

    barrier = pltpu.get_barrier_semaphore()
    for mask in range(1, n_tp):
        pl.semaphore_signal(barrier, inc=1, device_id={"tp": flip(tp, mask)}, device_id_type=MESH)
    for mask in range(1, n_ep):
        pl.semaphore_signal(barrier, inc=1, device_id={"ep": flip(ep, mask)}, device_id_type=MESH)
    back[...] = jnp.zeros_like(back)
    ids_out[...] = jnp.zeros_like(ids_out)
    acc[...] = jnp.zeros_like(acc)
    pl.semaphore_wait(barrier, n_tp + n_ep - 2)

    def piece(w, block, h):
        half = own_loads[w][0].shape[0] // 2
        rows = pl.ds(h * half, half)
        if w == 0:
            return tok_all.at[block, rows, :]
        return block_of([None, sg_in, su_in, sd_in][w], block, rows)

    def remote(source, target, send, recv, axis, place):
        return pltpu.make_async_remote_copy(
            src_ref=source,
            dst_ref=target,
            send_sem=send,
            recv_sem=recv,
            device_id={axis: place},
            device_id_type=MESH,
        )

    def ep_copy(w, h, mask, hop):
        ref = piece(w, flip(ep, mask), h)
        sem = (w, h, mask | hop)
        return remote(ref, ref, ep_send.at[sem], ep_recv.at[sem], "ep", flip(ep, hop))

    def ep_wait(w, h, mask):
        hop = [b for b in orders[h] if mask & b][-1]
        ref = piece(w, flip(ep, mask), h)
        sem = (w, h, mask)
        remote(ref, ref, ep_send.at[sem], ep_recv.at[sem], "ep", flip(ep, hop)).wait_recv()

    def ep_start(w):
        for position in range(len(orders[0])):
            for h in (0, 1):
                ep_copy(w, h, 0, orders[h][position]).start()

    def ep_level(w, masks):
        for mask in masks:
            for h in (0, 1):
                ep_wait(w, h, mask)
                for hop in later_hops(mask, orders[h]):
                    ep_copy(w, h, mask, hop).start()

    def tp_copy(mask, hop):
        ref = columns(own_rows, flip(tp, mask))
        source = tok_all.at[ep] if mask == 0 else ref
        sem = mask | hop
        return remote(source, ref, tp_send.at[sem], tp_recv.at[sem], "tp", flip(tp, hop))

    def tp_wait(mask):
        ref = columns(own_rows, flip(tp, mask))
        remote(ref, ref, tp_send.at[mask], tp_recv.at[mask], "tp", flip(tp, mask)).wait_recv()

    def used_piece(mask, h):
        cols = pl.ds(pl.multiple_of(flip(tp, mask) * width, width), width)
        return used_rows.at[pl.ds(*chunks[h]), cols]

    def disp_copy(mask, hop, h):
        source = used_piece(mask, h)
        if mask == 0:
            source = sel.at[flip(tp, hop) // split, pl.ds(*chunks[h]), :]
        sem = (mask | hop, h)
        return remote(
            source, used_piece(mask, h), disp_send.at[sem], disp_recv.at[sem], "tp", flip(tp, hop)
        )

    def disp_wait(mask, h):
        ref = used_piece(mask, h)
        sem = (mask, h)
        remote(ref, ref, disp_send.at[sem], disp_recv.at[sem], "tp", flip(tp, mask)).wait_recv()

    def low_hops(mask):
        return [b for b in bits_below(split) if b > mask % split]

    def hid_copy(mask, hop, h):
        ref = hidden.at[flip(tp, mask), :, pl.ds(*chunks[h])]
        sem = (mask | hop, h)
        return remote(ref, ref, hid_send.at[sem], hid_recv.at[sem], "tp", flip(tp, hop))

    def hid_wait(mask, h):
        ref = hidden.at[flip(tp, mask), :, pl.ds(*chunks[h])]
        sem = (mask, h)
        remote(ref, ref, hid_send.at[sem], hid_recv.at[sem], "tp", flip(tp, mask)).wait_recv()

    def up_copy(d):
        return remote(parts.at[d], in_up.at[d], up_send.at[d], up_recv.at[d], "tp", tp + 1)

    def down_copy(d):
        return remote(parts.at[d], in_down.at[d], down_send.at[d], down_recv.at[d], "tp", tp - 1)

    def up_wait(d):
        ref = in_up.at[d]
        remote(ref, ref, up_send.at[d], up_recv.at[d], "tp", tp - 1).wait_recv()

    def down_wait(d):
        ref = in_down.at[d]
        remote(ref, ref, down_send.at[d], down_recv.at[d], "tp", tp + 1).wait_recv()

    def ret_slot(k):
        return flip(tp, k * split) // split

    def ret_copy(mask, k):
        rows = pl.ds(0, slot_most)
        return remote(
            stage.at[k, flip(ep, mask)],
            back.at[k, ep, rows, :],
            ret_send.at[mask, k],
            ret_recv.at[mask, k],
            "ep",
            flip(ep, mask),
        )

    def ret_wait(mask, k):
        ref = back.at[k, flip(ep, mask), pl.ds(0, slot_most), :]
        sem = (mask, k)
        remote(ref, ref, ret_send.at[sem], ret_recv.at[sem], "ep", flip(ep, mask)).wait_recv()

    def ids_copy(mask):
        return remote(
            ids_out.at[flip(ep, mask)],
            ids_in.at[ep],
            ids_send_sem.at[mask],
            ids_recv_sem.at[mask],
            "ep",
            flip(ep, mask),
        )

    def ids_wait(mask):
        ref = ids_in.at[flip(ep, mask)]
        remote(
            ref, ref, ids_send_sem.at[mask], ids_recv_sem.at[mask], "ep", flip(ep, mask)
        ).wait_recv()

    loads[0].wait()
    ep_start(0)
    for hop in tp_order:
        tp_copy(0, hop).start()

    for s in range(n_exp):
        row = chosen_ref[pl.ds(s, 1), :]
        col = column_of(row.astype(f32), cap).astype(i32)
        chosen_col[s] = col
        gates_col[s] = column_of(gates_ref[pl.ds(s, 1), :], cap)
        row_from = jnp.zeros_like(row)
        col_from = jnp.zeros_like(col)
        for d in range(1, n_ep):
            row_from += jnp.where(row >= d * n_tok, 1, 0)
            col_from += jnp.where(col >= d * n_tok, 1, 0)
        ahead = jnp.where(col < row_from * n_tok, 1.0, 0.0)
        run_row = jnp.sum(ahead, axis=0, keepdims=True).astype(i32)
        ahead = jnp.where(row < col_from * n_tok, 1.0, 0.0)
        run_col = jnp.sum(ahead, axis=1, keepdims=True).astype(i32)
        lanes = lax.broadcasted_iota(i32, (1, cap), 1)
        rows = lax.broadcasted_iota(i32, (cap, 1), 0)
        place_row[s] = row_from * slot_most + lanes - run_row
        within = rows - run_col

        def slot_ids(d, carry):
            slots = lax.broadcasted_iota(i32, (cap, slot_pad), 1)
            wanted = jnp.where(col_from == d, within, -1)
            value = (col - d * n_tok + 1).astype(f32)
            total = jnp.sum(jnp.where(slots == wanted, value, 0.0), axis=0, keepdims=True)
            ids_out[d, pl.ds(s, 1), :] = total.astype(i32) - 1
            return carry

        lax.fori_loop(0, n_ep, slot_ids, 0)

    def select(e):
        def one(s, carry):
            ids = lax.broadcasted_iota(i32, (cap, n_tok), 1) + e * n_tok
            hits = jnp.where(chosen_col[s] == ids, 1.0, 0.0).astype(bf16)
            acc[s] += jnp.dot(hits, tok_all[e], preferred_element_type=f32)
            return carry

        lax.fori_loop(0, n_exp, one, 0)

    select(ep)
    ep_level(0, ep_levels[0])
    for load in loads[1:4]:
        load.wait()
    for w in (1, 2, 3):
        ep_start(w)
    ep_masks = sorted(range(1, n_ep), key=lambda m: -bin(m >> 1).count("1"))
    for mask in ep_masks:
        ids_copy(mask).start()
    ids_in[ep] = ids_out[ep]
    for mask in ep_levels[0]:
        select(flip(ep, mask))
    for masks in ep_levels[1:]:
        ep_level(0, masks)
        for mask in masks:
            select(flip(ep, mask))
    for s in range(n_exp):
        sel[s] = acc[s].astype(bf16)
    for h in parts_of:
        for hop in high_masks + low_hops(0):
            disp_copy(0, hop, h).start()
    own_used = pltpu.make_async_copy(sel.at[slot], columns(used_rows, tp), local_sem.at[8])
    own_used.start()
    acc[...] = jnp.zeros_like(acc)

    ep_level(1, ep_levels[0])
    for mask in high_masks:
        for h in parts_of:
            disp_wait(mask, h)
            for hop in low_hops(mask):
                disp_copy(mask, hop, h).start()
    ep_level(2, ep_levels[0])
    tp_rank = sorted(
        range(1, n_tp), key=lambda m: [tp_order.index(b) for b in tp_order if m & b][::-1]
    )
    first_tp = [m for m in tp_rank if m == tp_order[0]]
    for mask in first_tp:
        tp_wait(mask)
        for hop in later_hops(mask, tp_order):
            tp_copy(mask, hop).start()
    for mask in ep_masks:
        ids_wait(mask)
    for k in range(n_exp):
        for e in range(n_ep):
            ids = ids_in[e, pl.ds(ret_slot(k), 1), :]
            match = lax.broadcasted_iota(i32, (n_tok, slot_pad), 0) == ids
            picker[k, :, e * slot_pad : (e + 1) * slot_pad] = jnp.where(match, 1.0, 0.0).astype(bf16)
    ep_level(3, ep_levels[0])
    own_used.wait()
    loads[5].wait()
    loads[6].wait()
    low_masks = [m for m in range(1, n_tp) if m not in high_masks]
    for h in parts_of:
        for mask in low_masks:
            disp_wait(mask, h)
            for hop in low_hops(mask):
                disp_copy(mask, hop, h).start()
        used = normalise(used_rows[pl.ds(*chunks[h]), :], gain_ref[...])
        contract = (((1,), (1,)), ((), ()))
        gate = lax.dot_general(eg_ref[...], used, contract, preferred_element_type=f32)
        up = lax.dot_general(eu_ref[...], used, contract, preferred_element_type=f32)
        hidden[tp, :, pl.ds(*chunks[h])] = (jax.nn.silu(gate) * up).astype(bf16)
        for hop in tp_order[::-1]:
            hid_copy(0, hop, h).start()

    for masks in ep_levels[1:]:
        for w in (1, 2, 3):
            ep_level(w, masks)
    loads[4].wait()
    for mask in tp_rank:
        if mask not in first_tp:
            tp_wait(mask)
            for hop in later_hops(mask, tp_order):
                tp_copy(mask, hop).start()

    if flat:
        weights = flat
        cols = sg_hbm.shape[1]
        group = 128 // cols
        for ref, out in zip((sg_in, su_in, sd_in), flat):
            for j in range(n_ep // group):
                joined = jnp.concatenate([ref[j * group + i] for i in range(group)], axis=1)
                out[:, j * 128 : (j + 1) * 128] = joined
    else:
        weights = (sg_in, su_in, sd_in)
    sg_ref, su_ref, sd_ref = weights
    chunk = n_tok // 2

    def shared_rows(i, carry):
        rows = pl.ds(pl.multiple_of(i * chunk, chunk), chunk)
        x = normalise(own_rows[rows, :], gain_ref[...])
        contract = (((1,), (1,)), ((), ()))
        gate = lax.dot_general(x, sg_ref[...], contract, preferred_element_type=f32)
        up = lax.dot_general(x, su_ref[...], contract, preferred_element_type=f32)
        mid = (jax.nn.silu(gate) * up).astype(bf16)
        for block in range(n_tp):
            cols = pl.ds(block * width, width)
            parts[block, rows, :] = jnp.dot(
                mid, sd_ref[:, cols], preferred_element_type=f32
            ).astype(bf16)
        return carry

    lax.fori_loop(0, 2, shared_rows, 0)

    def sums_ends(j):
        @pl.when(tp == 0)
        def _():
            up_copy(n_tp - 1 - j).start()

        @pl.when(tp == n_tp - 1)
        def _():
            down_copy(j).start()

    def sums_middle(j):
        d = n_tp - 1 - j

        @pl.when(jnp.logical_and(tp > 0, tp < d))
        def _():
            up_wait(d)
            parts[d] = (parts[d].astype(f32) + in_up[d].astype(f32)).astype(bf16)
            up_copy(d).start()

        @pl.when(jnp.logical_and(tp < n_tp - 1, tp > j))
        def _():
            down_wait(j)
            parts[j] = (parts[j].astype(f32) + in_down[j].astype(f32)).astype(bf16)
            down_copy(j).start()

    def add_block(mask):
        block = flip(tp, mask)
        acc[block // split] += lax.dot_general(
            hidden[block], down_ref[block], (((0,), (0,)), ((), ())), preferred_element_type=f32
        )

    def give_back(k):
        s = ret_slot(k)
        weighted = (gates_col[s] * acc[s]).astype(bf16)
        slots = n_ep * slot_most
        placer = lax.broadcasted_iota(i32, (slots, cap), 0) == place_row[s]
        placer = jnp.where(placer, 1.0, 0.0).astype(bf16)
        placed = jnp.dot(placer, weighted, preferred_element_type=f32)
        stage[k] = placed.reshape(n_ep, slot_most, width).astype(bf16)
        for mask in ep_masks:
            ret_copy(mask, k).start()
        back[k, ep, :slot_most, :] = stage[k, ep]

    loads[7].wait()
    sums_ends(0)
    hid_masks = sorted(
        range(1, n_tp), key=lambda m: [tp_order.index(b) for b in tp_order if m & b][::-1]
    )
    hid_first = [m for m in hid_masks if m == tp_order[0]]
    for mask in hid_first:
        for h in parts_of:
            hid_wait(mask, h)
            for hop in later_hops(mask, tp_order):
                hid_copy(mask, hop, h).start()
    add_block(0)
    for k in range(n_exp):
        group = [m for m in hid_masks if m // split == k]
        for mask in group:
            if mask not in hid_first:
                for h in parts_of:
                    hid_wait(mask, h)
                    for hop in later_hops(mask, tp_order):
                        hid_copy(mask, hop, h).start()
            add_block(mask)
            if k > 0 and mask == group[0] and k == 1:
                for j in range(1, n_tp - 1):
                    sums_middle(j)
        give_back(k)
        if k == 0:
            for j in range(n_tp - 1):
                if j == 0:
                    sums_middle(0)
                if j > 0:
                    sums_ends(j)

    acc[0] = parts[tp].astype(f32)

    @pl.when(tp > 0)
    def _():
        up_wait(tp)
        acc[0] += in_up[tp].astype(f32)

    @pl.when(tp < n_tp - 1)
    def _():
        down_wait(tp)
        acc[0] += in_down[tp].astype(f32)

    for k in range(n_exp):
        for mask in ep_masks:
            ret_wait(mask, k)
        value = acc[0] + jnp.dot(
            picker[k], back[k].reshape(n_ep * slot_pad, width), preferred_element_type=f32
        )
        if k < n_exp - 1:
            acc[0] = value
        else:
            out_ref[...] = value.astype(bf16)

    for w in range(4):
        for h in (0, 1):
            for mask in range(n_ep):
                for hop in later_hops(mask, orders[h]):
                    ep_copy(w, h, mask, hop).wait_send()
    for mask in range(n_tp):
        for hop in later_hops(mask, tp_order):
            tp_copy(mask, hop).wait_send()
            for h in parts_of:
                hid_copy(mask, hop, h).wait_send()
    for mask in range(n_tp):
        hops = low_hops(mask)
        if mask == 0:
            hops = high_masks + hops
        for hop in hops:
            for h in parts_of:
                disp_copy(mask, hop, h).wait_send()
    for mask in ep_masks:
        ids_copy(mask).wait_send()
        for k in range(n_exp):
            ret_copy(mask, k).wait_send()
    for d in range(n_tp):

        @pl.when(tp < d)
        def _():
            up_copy(d).wait_send()

        @pl.when(tp > d)
        def _():
            down_copy(d).wait_send()


def on_device(
    tokens,
    norm_gain,
    shared_gate,
    shared_up,
    shared_down,
    expert_gate,
    expert_up,
    expert_down,
    chosen,
    gates,
):
    n_tp = lax.axis_size("tp")
    n_ep = lax.axis_size("ep")
    n_exp, cap = chosen.shape
    n_tok, width = tokens.shape
    model = n_tp * width
    bf16, f32, i32 = jnp.bfloat16, jnp.float32, jnp.int32
    slot_most = 2 * cap // n_ep
    slot_pad = -(-slot_most // 128) * 128
    n_hid = expert_gate.shape[2]
    sg, su, sd = shared_gate.T, shared_up.T, shared_down
    rows, cols = sg.shape
    if cols % 128 == 0:
        joined, flat = (rows, n_ep * cols), []
    else:
        joined = (n_ep, rows, cols)
        flat = [pltpu.VMEM((rows, n_ep * cols), bf16)] * 3
    vmem = pl.BlockSpec(memory_space=pltpu.VMEM)
    hbm = pl.BlockSpec(memory_space=pl.ANY)
    dma = pltpu.SemaphoreType.DMA
    return pl.pallas_call(
        functools.partial(layer_kernel, n_tp, n_ep, slot_most),
        out_shape=jax.ShapeDtypeStruct((n_tok, width), bf16),
        in_specs=[hbm, vmem] + [hbm] * 6 + [vmem] * 2,
        out_specs=vmem,
        scratch_shapes=[
            pltpu.VMEM((n_ep, n_tok, width), bf16),
            pltpu.VMEM((n_tok, model), bf16),
            pltpu.VMEM((cap, model), bf16),
            pltpu.VMEM((n_exp, cap, width), bf16),
            pltpu.VMEM(joined, bf16),
            pltpu.VMEM(joined, bf16),
            pltpu.VMEM(joined, bf16),
            pltpu.VMEM((n_hid, model), bf16),
            pltpu.VMEM((n_hid, model), bf16),
            pltpu.VMEM((n_tp, n_hid, width), bf16),
            pltpu.VMEM((n_tp, n_hid, cap), bf16),
            pltpu.VMEM((n_exp, cap, width), f32),
            pltpu.VMEM((n_tp, n_tok, width), bf16),
            pltpu.VMEM((n_tp, n_tok, width), bf16),
            pltpu.VMEM((n_tp, n_tok, width), bf16),
            pltpu.VMEM((n_exp, n_ep, slot_most, width), bf16),
            pltpu.VMEM((n_exp, n_ep, slot_pad, width), bf16),
            pltpu.VMEM((n_exp, n_tok, n_ep * slot_pad), bf16),
            pltpu.VMEM((n_ep, 8, slot_pad), i32),
            pltpu.VMEM((n_ep, 8, slot_pad), i32),
            pltpu.VMEM((n_exp, cap, 1), i32),
            pltpu.VMEM((n_exp, cap, 1), f32),
            pltpu.VMEM((n_exp, 1, cap), i32),
            dma((4, 2, n_ep)),
            dma((4, 2, n_ep)),
            dma((n_tp,)),
            dma((n_tp,)),
            dma((n_tp, 2)),
            dma((n_tp, 2)),
            dma((n_tp, 2)),
            dma((n_tp, 2)),
            dma((n_tp,)),
            dma((n_tp,)),
            dma((n_tp,)),
            dma((n_tp,)),
            dma((n_ep, n_exp)),
            dma((n_ep, n_exp)),
            dma((n_ep,)),
            dma((n_ep,)),
            dma((9,)),
        ]
        + flat,
        compiler_params=pltpu.CompilerParams(
            collective_id=0, has_side_effects=True, vmem_limit_bytes=62 * 1024 * 1024
        ),
    )(
        tokens,
        norm_gain.reshape(1, -1),
        sg,
        su,
        sd,
        expert_gate.reshape(n_hid, model),
        expert_up.reshape(n_hid, model),
        expert_down.reshape(n_tp, n_hid, width),
        chosen,
        gates,
    )


def solution(mesh):
    return jax.shard_map(
        on_device,
        mesh=mesh,
        in_specs=(
            P("ep", "tp"),
            P(),
            P("ep", "tp"),
            P("ep", "tp"),
            P("tp", "ep"),
            P("tp", "ep", None, None),
            P("tp", "ep", None, None),
            P("ep", None, "tp"),
            P("ep", None),
            P("ep", None),
        ),
        out_specs=P("ep", "tp"),
        check_vma=False,
    )
```

time: 157 us -> 127 us (0.81)
  Pallas kernels: 136 us -> 123 us
  local copies, waits for them, and re-layouts: 9.86 us -> 1.77 us
  other arithmetic: 5.15 us -> 0 us
  matrix products: 4.38 us -> 0 us
    pallas_call x2 -> x1, Pallas kernels: 136 us -> 123 us  [on_device(): pl.pallas_call(functools.partial(layer_kernel, n_tp, n_ep, slot_most), ou...]
    unnamed x23 -> x1, local copies, waits for them, and re-layouts: 6.46 us -> 1.77 us
    dot_general x2 -> x0, matrix products: 4.38 us -> none  [the longest x1 2.62 us: on_device(): jnp.einsum('hd,rd->hr', up_weight, used, preferred_element_type=f32)]
    convert_element_type x1 -> x0, other arithmetic: 3.05 us -> none  [normalise(): return (widened * inv_scale * gain).astype(jnp.bfloat16)]
    broadcast_in_dim x3 -> x0, local copies, waits for them, and re-layouts: 2.54 us -> none  [the longest x1 1.01 us: upfront(): chosen[:, :, None]]
    reduce_sum x4 -> x0, other arithmetic: 1.99 us -> none  [the longest x1 0.69 us: normalise(): jnp.mean(widened * widened, axis=1, keepdims=True) + norm_eps]
where the time goes in v1:
time: 127 us; the launch traced here: 125 us
  Pallas kernels  123 us (97%)
  local copies, waits for them, and re-layouts  1.77 us (1%)
    pallas_call x1, Pallas kernels, on_device(): pl.pallas_call(functools.partial(layer_kernel, n_tp, n_ep, slot_most), ou...  123 us

profile of v1, /device:TPU:0, one launch (start us, length us, event | category | flops | bytes accessed | tf_op | source)
XLA Modules:
  0.0 124.6 jit_solution(5241903549271508613)
XLA Ops:
  0.0 122.8 %shard_map.100 = bf16[384,512]{1,0:T(8,128)(2,1)} custom-call(bf16[384,512]{1,0:T(8,128)(2,1)} %tok_hbm.1, f32[1,2048]{1,0:T(1,128)} %bitcast.11, bf16[704,256]{1,0:T(8,128)(2,1)} %bitcast.9, bf16[704,256]{1,0:T(8,128)(2,1)} %bitcast.10, bf16[704,256]{1,0:T(8,128)(2,1)} %sd_hbm.1, bf16[704,2048]{1,0:T(8,128)(2,1)} %bitcast.6, bf16[704,2048]{1,0:T(8,128)(2,1)} %bitcast.7, ...), custom_call_target="tpu_custom_call" | custom-call | tf_op jit(solution)/shard_map/pallas_call | solution.py:611
  122.8 1.8 %copy.12 = bf16[384,512]{1,0:T(8,128)(2,1)} copy(bf16[384,512]{1,0:T(8,128)(2,1)} %shard_map.100) | data formatting | bytes 786432

commit v2 on v1

--- a/solution.py
+++ b/solution.py
@@ -104,6 +104,7 @@
     tp_recv,
     disp_send,
     disp_recv,
+    far_send,
     hid_send,
     hid_recv,
     up_send,
@@ -127,8 +128,6 @@
     split = n_tp // n_exp
     slot = tp // split
     orders = half_orders(n_ep)
-    high_masks = [k * split for k in range(1, n_exp)]
-    tp_order = bits_below(n_tp)[::-1]
     ep_levels = levels(n_ep)
     cut = max(128, cap * 2 // 3 // 128 * 128)
     chunks = [(0, cut), (cut, cap - cut)]
@@ -211,46 +210,152 @@
                 for hop in later_hops(mask, orders[h]):
                     ep_copy(w, h, mask, hop).start()
 
-    def tp_copy(mask, hop):
-        ref = columns(own_rows, flip(tp, mask))
-        source = tok_all.at[ep] if mask == 0 else ref
-        sem = mask | hop
-        return remote(source, ref, tp_send.at[sem], tp_recv.at[sem], "tp", flip(tp, hop))
-
-    def tp_wait(mask):
-        ref = columns(own_rows, flip(tp, mask))
-        remote(ref, ref, tp_send.at[mask], tp_recv.at[mask], "tp", flip(tp, mask)).wait_recv()
-
-    def used_piece(mask, h):
-        cols = pl.ds(pl.multiple_of(flip(tp, mask) * width, width), width)
+    def known(up, j):
+        return tp >= j if up else tp < n_tp - j
+
+    def ahead(up):
+        return tp < n_tp - 1 if up else tp > 0
+
+    def at_distance(up, j):
+        return tp - j if up else tp + j
+
+    def tok_ref(ref, block, h):
+        half = n_tok // 2
+        cols = pl.ds(pl.multiple_of(block * width, width), width)
+        return ref.at[pl.ds(h * half, half), cols]
+
+    def tok_copy(up, j, h):
+        ref = tok_ref(own_rows, at_distance(up, j), h)
+        source = tok_all.at[ep, pl.ds(h * (n_tok // 2), n_tok // 2), :] if j == 0 else ref
+        sem = (up, j, h)
+        return remote(
+            source, ref, tp_send.at[sem], tp_recv.at[sem], "tp", at_distance(1 - up, 1)
+        )
+
+    def tok_wait(up, j, h):
+        ref = tok_ref(own_rows, at_distance(up, j), h)
+        sem = (up, j - 1, h)
+        remote(ref, ref, tp_send.at[sem], tp_recv.at[sem], "tp", at_distance(up, 1)).wait_recv()
+
+    def hid_copy(up, j, h):
+        ref = hidden.at[at_distance(up, j), :, pl.ds(*chunks[h])]
+        sem = (up, j, h)
+        return remote(
+            ref, ref, hid_send.at[sem], hid_recv.at[sem], "tp", at_distance(1 - up, 1)
+        )
+
+    def hid_wait(up, j, h):
+        ref = hidden.at[at_distance(up, j), :, pl.ds(*chunks[h])]
+        sem = (up, j - 1, h)
+        remote(ref, ref, hid_send.at[sem], hid_recv.at[sem], "tp", at_distance(up, 1)).wait_recv()
+
+    def line_start(copy, *rest):
+        for up in (0, 1):
+
+            @pl.when(ahead(up))
+            def _():
+                copy(up, 0, *rest).start()
+
+    def line_pass(copy, wait, j, *rest, side=None):
+        for up in (0, 1):
+            here = known(up, j)
+            if side is not None:
+                near = tp < n_tp // 2 if up == side else tp >= n_tp // 2
+                here = jnp.logical_and(here, near)
+
+            @pl.when(here)
+            def _():
+                wait(up, j, *rest)
+
+                @pl.when(ahead(up))
+                def _():
+                    copy(up, j, *rest).start()
+
+    def hid_pass(j, side):
+        for h in parts_of:
+            line_pass(hid_copy, hid_wait, j, h, side=side)
+
+    def tok_pass(j, h):
+        line_pass(tok_copy, tok_wait, j, h)
+
+    def ret_slot(k):
+        return flip(tp, k * split) // split
+
+    low = slot * split
+    top = low + split - 1
+
+    def in_group(up):
+        return tp < top if up else tp > low
+
+    def used_piece(block, h):
+        cols = pl.ds(pl.multiple_of(block * width, width), width)
         return used_rows.at[pl.ds(*chunks[h]), cols]
 
-    def disp_copy(mask, hop, h):
-        source = used_piece(mask, h)
-        if mask == 0:
-            source = sel.at[flip(tp, hop) // split, pl.ds(*chunks[h]), :]
-        sem = (mask | hop, h)
+    def disp_copy(up, j, h):
+        block = at_distance(up, j)
+        ref = used_piece(block, h)
+        source = sel.at[slot, pl.ds(*chunks[h]), :] if j == 0 else ref
         return remote(
-            source, used_piece(mask, h), disp_send.at[sem], disp_recv.at[sem], "tp", flip(tp, hop)
-        )
-
-    def disp_wait(mask, h):
-        ref = used_piece(mask, h)
-        sem = (mask, h)
-        remote(ref, ref, disp_send.at[sem], disp_recv.at[sem], "tp", flip(tp, mask)).wait_recv()
-
-    def low_hops(mask):
-        return [b for b in bits_below(split) if b > mask % split]
-
-    def hid_copy(mask, hop, h):
-        ref = hidden.at[flip(tp, mask), :, pl.ds(*chunks[h])]
-        sem = (mask | hop, h)
-        return remote(ref, ref, hid_send.at[sem], hid_recv.at[sem], "tp", flip(tp, hop))
-
-    def hid_wait(mask, h):
-        ref = hidden.at[flip(tp, mask), :, pl.ds(*chunks[h])]
-        sem = (mask, h)
-        remote(ref, ref, hid_send.at[sem], hid_recv.at[sem], "tp", flip(tp, mask)).wait_recv()
+            source,
+            ref,
+            disp_send.at[up, j, h],
+            disp_recv.at[block, h],
+            "tp",
+            at_distance(1 - up, 1),
+        )
+
+    def disp_wait(up, j, h):
+        block = at_distance(up, j)
+        ref = used_piece(block, h)
+        remote(
+            ref, ref, disp_send.at[up, j, h], disp_recv.at[block, h], "tp", at_distance(up, 1)
+        ).wait_recv()
+
+    def far_copy(k, h, entry):
+        return remote(
+            sel.at[ret_slot(k), pl.ds(*chunks[h]), :],
+            used_piece(tp, h),
+            far_send.at[k, h],
+            disp_recv.at[tp, h],
+            "tp",
+            entry,
+        )
+
+    def far_each(act, h):
+        for k in range(1, n_exp):
+            s = ret_slot(k)
+
+            @pl.when(s > slot)
+            def _():
+                act(far_copy(k, h, s * split))
+
+            @pl.when(s < slot)
+            def _():
+                act(far_copy(k, h, s * split + split - 1))
+
+    def disp_start(h):
+        far_each(lambda copy: copy.start(), h)
+        for up in (0, 1):
+
+            @pl.when(in_group(up))
+            def _():
+                disp_copy(up, 0, h).start()
+
+    def disp_pass(j, h):
+        for up in (0, 1):
+
+            @pl.when(jnp.logical_and(known(up, j), in_group(up)))
+            def _():
+                disp_wait(up, j, h)
+                disp_copy(up, j, h).start()
+
+    def disp_rest(h):
+        for j in range(1, n_tp):
+            for up in (0, 1):
+
+                @pl.when(jnp.logical_and(known(up, j), jnp.logical_not(in_group(up))))
+                def _():
+                    disp_wait(up, j, h)
 
     def up_copy(d):
         return remote(parts.at[d], in_up.at[d], up_send.at[d], up_recv.at[d], "tp", tp + 1)
@@ -265,9 +370,6 @@
     def down_wait(d):
         ref = in_down.at[d]
         remote(ref, ref, down_send.at[d], down_recv.at[d], "tp", tp + 1).wait_recv()
-
-    def ret_slot(k):
-        return flip(tp, k * split) // split
 
     def ret_copy(mask, k):
         rows = pl.ds(0, slot_most)
@@ -303,8 +405,8 @@
 
     loads[0].wait()
     ep_start(0)
-    for hop in tp_order:
-        tp_copy(0, hop).start()
+    for h in (0, 1):
+        line_start(tok_copy, h)
 
     for s in range(n_exp):
         row = chosen_ref[pl.ds(s, 1), :]
@@ -316,10 +418,10 @@
         for d in range(1, n_ep):
             row_from += jnp.where(row >= d * n_tok, 1, 0)
             col_from += jnp.where(col >= d * n_tok, 1, 0)
-        ahead = jnp.where(col < row_from * n_tok, 1.0, 0.0)
-        run_row = jnp.sum(ahead, axis=0, keepdims=True).astype(i32)
-        ahead = jnp.where(row < col_from * n_tok, 1.0, 0.0)
-        run_col = jnp.sum(ahead, axis=1, keepdims=True).astype(i32)
+        before = jnp.where(col < row_from * n_tok, 1.0, 0.0)
+        run_row = jnp.sum(before, axis=0, keepdims=True).astype(i32)
+        before = jnp.where(row < col_from * n_tok, 1.0, 0.0)
+        run_col = jnp.sum(before, axis=1, keepdims=True).astype(i32)
         lanes = lax.broadcasted_iota(i32, (1, cap), 1)
         rows = lax.broadcasted_iota(i32, (cap, 1), 0)
         place_row[s] = row_from * slot_most + lanes - run_row
@@ -345,6 +447,8 @@
         lax.fori_loop(0, n_exp, one, 0)
 
     select(ep)
+    if n_tp > 2:
+        tok_pass(1, 0)
     ep_level(0, ep_levels[0])
     for load in loads[1:4]:
         load.wait()
@@ -354,36 +458,34 @@
     for mask in ep_masks:
         ids_copy(mask).start()
     ids_in[ep] = ids_out[ep]
+    if n_tp > 2:
+        tok_pass(1, 1)
     for mask in ep_levels[0]:
         select(flip(ep, mask))
+    if n_tp > 3:
+        tok_pass(2, 0)
     for masks in ep_levels[1:]:
-        ep_level(0, masks)
-        for mask in masks:
+        for mask in sorted(masks, key=lambda m: -(m % 2)):
+            ep_level(0, [mask])
             select(flip(ep, mask))
     for s in range(n_exp):
         sel[s] = acc[s].astype(bf16)
-    for h in parts_of:
-        for hop in high_masks + low_hops(0):
-            disp_copy(0, hop, h).start()
+    disp_start(0)
     own_used = pltpu.make_async_copy(sel.at[slot], columns(used_rows, tp), local_sem.at[8])
     own_used.start()
     acc[...] = jnp.zeros_like(acc)
-
+    if n_tp > 3:
+        tok_pass(2, 1)
+    for j in range(3, n_tp - 1):
+        for h in (0, 1):
+            tok_pass(j, h)
     ep_level(1, ep_levels[0])
-    for mask in high_masks:
-        for h in parts_of:
-            disp_wait(mask, h)
-            for hop in low_hops(mask):
-                disp_copy(mask, hop, h).start()
+    disp_start(1)
+    for j in range(1, n_tp):
+        disp_pass(j, 0)
     ep_level(2, ep_levels[0])
-    tp_rank = sorted(
-        range(1, n_tp), key=lambda m: [tp_order.index(b) for b in tp_order if m & b][::-1]
-    )
-    first_tp = [m for m in tp_rank if m == tp_order[0]]
-    for mask in first_tp:
-        tp_wait(mask)
-        for hop in later_hops(mask, tp_order):
-            tp_copy(mask, hop).start()
+    for j in range(1, n_tp):
+        disp_pass(j, 1)
     for mask in ep_masks:
         ids_wait(mask)
     for k in range(n_exp):
@@ -395,30 +497,21 @@
     own_used.wait()
     loads[5].wait()
     loads[6].wait()
-    low_masks = [m for m in range(1, n_tp) if m not in high_masks]
     for h in parts_of:
-        for mask in low_masks:
-            disp_wait(mask, h)
-            for hop in low_hops(mask):
-                disp_copy(mask, hop, h).start()
+        disp_rest(h)
         used = normalise(used_rows[pl.ds(*chunks[h]), :], gain_ref[...])
         contract = (((1,), (1,)), ((), ()))
         gate = lax.dot_general(eg_ref[...], used, contract, preferred_element_type=f32)
         up = lax.dot_general(eu_ref[...], used, contract, preferred_element_type=f32)
         hidden[tp, :, pl.ds(*chunks[h])] = (jax.nn.silu(gate) * up).astype(bf16)
-        for hop in tp_order[::-1]:
-            hid_copy(0, hop, h).start()
-
+        line_start(hid_copy, h)
     for masks in ep_levels[1:]:
         for w in (1, 2, 3):
             ep_level(w, masks)
     loads[4].wait()
-    for mask in tp_rank:
-        if mask not in first_tp:
-            tp_wait(mask)
-            for hop in later_hops(mask, tp_order):
-                tp_copy(mask, hop).start()
-
+    for h in (0, 1):
+        tok_pass(n_tp - 1, h)
+    hid_pass(1, 0)
     if flat:
         weights = flat
         cols = sg_hbm.shape[1]
@@ -492,36 +585,20 @@
 
     loads[7].wait()
     sums_ends(0)
-    hid_masks = sorted(
-        range(1, n_tp), key=lambda m: [tp_order.index(b) for b in tp_order if m & b][::-1]
-    )
-    hid_first = [m for m in hid_masks if m == tp_order[0]]
-    for mask in hid_first:
-        for h in parts_of:
-            hid_wait(mask, h)
-            for hop in later_hops(mask, tp_order):
-                hid_copy(mask, hop, h).start()
     add_block(0)
-    for k in range(n_exp):
-        group = [m for m in hid_masks if m // split == k]
-        for mask in group:
-            if mask not in hid_first:
-                for h in parts_of:
-                    hid_wait(mask, h)
-                    for hop in later_hops(mask, tp_order):
-                        hid_copy(mask, hop, h).start()
-            add_block(mask)
-            if k > 0 and mask == group[0] and k == 1:
-                for j in range(1, n_tp - 1):
-                    sums_middle(j)
-        give_back(k)
-        if k == 0:
-            for j in range(n_tp - 1):
-                if j == 0:
-                    sums_middle(0)
-                if j > 0:
-                    sums_ends(j)
-
+    hid_pass(1, 1)
+    for j in range(1, n_tp):
+        if j > 1:
+            hid_pass(j, 0)
+            hid_pass(j, 1)
+        add_block(j)
+        if (j + 1) % split == 0:
+            give_back(j // split)
+        if j > 1:
+            sums_middle(j - 2)
+        if j < n_tp - 1:
+            sums_ends(j)
+    sums_middle(n_tp - 2)
     acc[0] = parts[tp].astype(f32)
 
     @pl.when(tp > 0)
@@ -550,18 +627,24 @@
             for mask in range(n_ep):
                 for hop in later_hops(mask, orders[h]):
                     ep_copy(w, h, mask, hop).wait_send()
-    for mask in range(n_tp):
-        for hop in later_hops(mask, tp_order):
-            tp_copy(mask, hop).wait_send()
-            for h in parts_of:
-                hid_copy(mask, hop, h).wait_send()
-    for mask in range(n_tp):
-        hops = low_hops(mask)
-        if mask == 0:
-            hops = high_masks + hops
-        for hop in hops:
-            for h in parts_of:
-                disp_copy(mask, hop, h).wait_send()
+    for h in parts_of:
+        far_each(lambda copy: copy.wait_send(), h)
+    for up in (0, 1):
+        for j in range(n_tp - 1):
+
+            @pl.when(jnp.logical_and(known(up, j), ahead(up)))
+            def _():
+                for h in parts_of:
+                    tok_copy(up, j, h).wait_send()
+                    hid_copy(up, j, h).wait_send()
+
+        for j in range(n_tp):
+
+            @pl.when(jnp.logical_and(known(up, j), in_group(up)))
+            def _():
+                for h in parts_of:
+                    disp_copy(up, j, h).wait_send()
+
     for mask in ep_masks:
         ids_copy(mask).wait_send()
         for k in range(n_exp):
@@ -639,12 +722,13 @@
             pltpu.VMEM((n_exp, 1, cap), i32),
             dma((4, 2, n_ep)),
             dma((4, 2, n_ep)),
-            dma((n_tp,)),
-            dma((n_tp,)),
+            dma((2, n_tp, 2)),
+            dma((2, n_tp, 2)),
+            dma((2, n_tp, 2)),
             dma((n_tp, 2)),
-            dma((n_tp, 2)),
-            dma((n_tp, 2)),
-            dma((n_tp, 2)),
+            dma((n_exp, 2)),
+            dma((2, n_tp, 2)),
+            dma((2, n_tp, 2)),
             dma((n_tp,)),
             dma((n_tp,)),
             dma((n_tp,)),

time: 127 us -> 119 us (0.937); the launches traced: 125 us -> 119 us
  Pallas kernels: 123 us -> 117 us
    pallas_call x1, Pallas kernels: 123 us -> 117 us  [on_device(): pl.pallas_call(functools.partial(layer_kernel, n_tp, n_ep, slot_most), ou...]
where the time goes in v2:
time: 119 us
  Pallas kernels  117 us (98%)
  local copies, waits for them, and re-layouts  1.77 us (1%)
    pallas_call x1, Pallas kernels, on_device(): pl.pallas_call(functools.partial(layer_kernel, n_tp, n_ep, slot_most), ou...  117 us

profile of v2, /device:TPU:0, one launch (start us, length us, event | category | flops | bytes accessed | tf_op | source)
XLA Modules:
  0.0 118.7 jit_solution(15530717457040168353)
XLA Ops:
  0.0 117.0 %shard_map.100 = bf16[384,512]{1,0:T(8,128)(2,1)} custom-call(bf16[384,512]{1,0:T(8,128)(2,1)} %tok_hbm.1, f32[1,2048]{1,0:T(1,128)} %bitcast.11, bf16[704,256]{1,0:T(8,128)(2,1)} %bitcast.9, bf16[704,256]{1,0:T(8,128)(2,1)} %bitcast.10, bf16[704,256]{1,0:T(8,128)(2,1)} %sd_hbm.1, bf16[704,2048]{1,0:T(8,128)(2,1)} %bitcast.6, bf16[704,2048]{1,0:T(8,128)(2,1)} %bitcast.7, ...), custom_call_target="tpu_custom_call" | custom-call | tf_op jit(solution)/shard_map/pallas_call | solution.py:694
  117.0 1.8 %copy.12 = bf16[384,512]{1,0:T(8,128)(2,1)} copy(bf16[384,512]{1,0:T(8,128)(2,1)} %shard_map.100) | data formatting | bytes 786432

commit v3 on v2

--- a/solution.py
+++ b/solution.py
@@ -511,7 +511,6 @@
     loads[4].wait()
     for h in (0, 1):
         tok_pass(n_tp - 1, h)
-    hid_pass(1, 0)
     if flat:
         weights = flat
         cols = sg_hbm.shape[1]
@@ -550,7 +549,7 @@
         def _():
             down_copy(j).start()
 
-    def sums_middle(j):
+    def sums_up(j):
         d = n_tp - 1 - j
 
         @pl.when(jnp.logical_and(tp > 0, tp < d))
@@ -559,11 +558,23 @@
             parts[d] = (parts[d].astype(f32) + in_up[d].astype(f32)).astype(bf16)
             up_copy(d).start()
 
+    def sums_down(j):
         @pl.when(jnp.logical_and(tp < n_tp - 1, tp > j))
         def _():
             down_wait(j)
             parts[j] = (parts[j].astype(f32) + in_down[j].astype(f32)).astype(bf16)
             down_copy(j).start()
+
+    def sums_middle(j):
+        @pl.when(tp < n_tp // 2)
+        def _():
+            sums_up(j)
+            sums_down(j)
+
+        @pl.when(tp >= n_tp // 2)
+        def _():
+            sums_down(j)
+            sums_up(j)
 
     def add_block(mask):
         block = flip(tp, mask)
@@ -586,6 +597,7 @@
     loads[7].wait()
     sums_ends(0)
     add_block(0)
+    hid_pass(1, 0)
     hid_pass(1, 1)
     for j in range(1, n_tp):
         if j > 1:

time: 119 us -> 109 us (0.916)
  Pallas kernels: 117 us -> 107 us
    pallas_call x1, Pallas kernels: 117 us -> 107 us  [on_device(): pl.pallas_call(functools.partial(layer_kernel, n_tp, n_ep, slot_most), ou...]
where the time goes in v3:
time: 109 us; the launch traced here: 108 us
  Pallas kernels  107 us (98%)
  local copies, waits for them, and re-layouts  1.77 us (2%)
    pallas_call x1, Pallas kernels, on_device(): pl.pallas_call(functools.partial(layer_kernel, n_tp, n_ep, slot_most), ou...  107 us

profile of v3, /device:TPU:0, one launch (start us, length us, event | category | flops | bytes accessed | tf_op | source)
XLA Modules:
  0.0 108.4 jit_solution(12288094779511912165)
XLA Ops:
  0.0 106.6 %shard_map.100 = bf16[384,512]{1,0:T(8,128)(2,1)} custom-call(bf16[384,512]{1,0:T(8,128)(2,1)} %tok_hbm.1, f32[1,2048]{1,0:T(1,128)} %bitcast.11, bf16[704,256]{1,0:T(8,128)(2,1)} %bitcast.9, bf16[704,256]{1,0:T(8,128)(2,1)} %bitcast.10, bf16[704,256]{1,0:T(8,128)(2,1)} %sd_hbm.1, bf16[704,2048]{1,0:T(8,128)(2,1)} %bitcast.6, bf16[704,2048]{1,0:T(8,128)(2,1)} %bitcast.7, ...), custom_call_target="tpu_custom_call" | custom-call | tf_op jit(solution)/shard_map/pallas_call | solution.py:706
  106.6 1.8 %copy.12 = bf16[384,512]{1,0:T(8,128)(2,1)} copy(bf16[384,512]{1,0:T(8,128)(2,1)} %shard_map.100) | data formatting | bytes 786432

commit v4 on v3

--- a/solution.py
+++ b/solution.py
@@ -65,16 +65,20 @@
     n_ep,
     slot_most,
     tok_hbm,
-    gain_ref,
+    gain_hbm,
     sg_hbm,
     su_hbm,
     sd_hbm,
     eg_hbm,
     eu_hbm,
     down_hbm,
+    chosen_hbm,
+    gates_hbm,
+    out_hbm,
+    out_ref,
+    gain_ref,
     chosen_ref,
     gates_ref,
-    out_ref,
     tok_all,
     own_rows,
     used_rows,
@@ -157,6 +161,9 @@
     loads.append(pltpu.make_async_copy(tok_hbm, columns(own_rows, tp), local_sem.at[4]))
     for i, (source, target) in enumerate(((eg_hbm, eg_ref), (eu_hbm, eu_ref), (down_hbm, down_ref))):
         loads.append(pltpu.make_async_copy(source, target, local_sem.at[5 + i]))
+    small = ((chosen_hbm, chosen_ref), (gates_hbm, gates_ref), (gain_hbm, gain_ref))
+    for i, (source, target) in enumerate(small):
+        loads.append(pltpu.make_async_copy(source, target, local_sem.at[10 + i]))
     for load in loads:
         load.start()
 
@@ -189,14 +196,14 @@
 
     def ep_copy(w, h, mask, hop):
         ref = piece(w, flip(ep, mask), h)
-        sem = (w, h, mask | hop)
-        return remote(ref, ref, ep_send.at[sem], ep_recv.at[sem], "ep", flip(ep, hop))
+        sem = (w, h, (mask | hop) - 1)
+        return remote(ref, ref, ep_send.at[w], ep_recv.at[sem], "ep", flip(ep, hop))
 
     def ep_wait(w, h, mask):
         hop = [b for b in orders[h] if mask & b][-1]
         ref = piece(w, flip(ep, mask), h)
-        sem = (w, h, mask)
-        remote(ref, ref, ep_send.at[sem], ep_recv.at[sem], "ep", flip(ep, hop)).wait_recv()
+        sem = (w, h, mask - 1)
+        remote(ref, ref, ep_send.at[w], ep_recv.at[sem], "ep", flip(ep, hop)).wait_recv()
 
     def ep_start(w):
         for position in range(len(orders[0])):
@@ -229,25 +236,25 @@
         source = tok_all.at[ep, pl.ds(h * (n_tok // 2), n_tok // 2), :] if j == 0 else ref
         sem = (up, j, h)
         return remote(
-            source, ref, tp_send.at[sem], tp_recv.at[sem], "tp", at_distance(1 - up, 1)
+            source, ref, tp_send.at[up], tp_recv.at[sem], "tp", at_distance(1 - up, 1)
         )
 
     def tok_wait(up, j, h):
         ref = tok_ref(own_rows, at_distance(up, j), h)
         sem = (up, j - 1, h)
-        remote(ref, ref, tp_send.at[sem], tp_recv.at[sem], "tp", at_distance(up, 1)).wait_recv()
+        remote(ref, ref, tp_send.at[up], tp_recv.at[sem], "tp", at_distance(up, 1)).wait_recv()
 
     def hid_copy(up, j, h):
         ref = hidden.at[at_distance(up, j), :, pl.ds(*chunks[h])]
         sem = (up, j, h)
         return remote(
-            ref, ref, hid_send.at[sem], hid_recv.at[sem], "tp", at_distance(1 - up, 1)
+            ref, ref, hid_send.at[up], hid_recv.at[sem], "tp", at_distance(1 - up, 1)
         )
 
     def hid_wait(up, j, h):
         ref = hidden.at[at_distance(up, j), :, pl.ds(*chunks[h])]
         sem = (up, j - 1, h)
-        remote(ref, ref, hid_send.at[sem], hid_recv.at[sem], "tp", at_distance(up, 1)).wait_recv()
+        remote(ref, ref, hid_send.at[up], hid_recv.at[sem], "tp", at_distance(up, 1)).wait_recv()
 
     def line_start(copy, *rest):
         for up in (0, 1):
@@ -298,7 +305,7 @@
         return remote(
             source,
             ref,
-            disp_send.at[up, j, h],
+            disp_send.at[up],
             disp_recv.at[block, h],
             "tp",
             at_distance(1 - up, 1),
@@ -308,14 +315,14 @@
         block = at_distance(up, j)
         ref = used_piece(block, h)
         remote(
-            ref, ref, disp_send.at[up, j, h], disp_recv.at[block, h], "tp", at_distance(up, 1)
+            ref, ref, disp_send.at[up], disp_recv.at[block, h], "tp", at_distance(up, 1)
         ).wait_recv()
 
     def far_copy(k, h, entry):
         return remote(
             sel.at[ret_slot(k), pl.ds(*chunks[h]), :],
             used_piece(tp, h),
-            far_send.at[k, h],
+            far_send.at[0],
             disp_recv.at[tp, h],
             "tp",
             entry,
@@ -358,56 +365,56 @@
                     disp_wait(up, j, h)
 
     def up_copy(d):
-        return remote(parts.at[d], in_up.at[d], up_send.at[d], up_recv.at[d], "tp", tp + 1)
+        return remote(parts.at[d], in_up.at[d], up_send.at[0], up_recv.at[d], "tp", tp + 1)
 
     def down_copy(d):
-        return remote(parts.at[d], in_down.at[d], down_send.at[d], down_recv.at[d], "tp", tp - 1)
+        return remote(parts.at[d], in_down.at[d], down_send.at[0], down_recv.at[d], "tp", tp - 1)
 
     def up_wait(d):
         ref = in_up.at[d]
-        remote(ref, ref, up_send.at[d], up_recv.at[d], "tp", tp - 1).wait_recv()
+        remote(ref, ref, up_send.at[0], up_recv.at[d], "tp", tp - 1).wait_recv()
 
     def down_wait(d):
         ref = in_down.at[d]
-        remote(ref, ref, down_send.at[d], down_recv.at[d], "tp", tp + 1).wait_recv()
+        remote(ref, ref, down_send.at[0], down_recv.at[d], "tp", tp + 1).wait_recv()
 
     def ret_copy(mask, k):
         rows = pl.ds(0, slot_most)
         return remote(
             stage.at[k, flip(ep, mask)],
             back.at[k, ep, rows, :],
-            ret_send.at[mask, k],
-            ret_recv.at[mask, k],
+            ret_send.at[k],
+            ret_recv.at[k],
             "ep",
             flip(ep, mask),
         )
 
-    def ret_wait(mask, k):
-        ref = back.at[k, flip(ep, mask), pl.ds(0, slot_most), :]
-        sem = (mask, k)
-        remote(ref, ref, ret_send.at[sem], ret_recv.at[sem], "ep", flip(ep, mask)).wait_recv()
+    def local_wait(ref, sem):
+        pltpu.make_async_copy(ref, ref, sem).wait()
+
+    def ret_wait(k):
+        local_wait(back.at[k, pl.ds(0, n_ep - 1), pl.ds(0, slot_most), :], ret_recv.at[k])
 
     def ids_copy(mask):
         return remote(
             ids_out.at[flip(ep, mask)],
             ids_in.at[ep],
-            ids_send_sem.at[mask],
-            ids_recv_sem.at[mask],
+            ids_send_sem.at[0],
+            ids_recv_sem.at[0],
             "ep",
             flip(ep, mask),
         )
 
-    def ids_wait(mask):
-        ref = ids_in.at[flip(ep, mask)]
-        remote(
-            ref, ref, ids_send_sem.at[mask], ids_recv_sem.at[mask], "ep", flip(ep, mask)
-        ).wait_recv()
+    def ids_wait():
+        local_wait(ids_in.at[pl.ds(0, n_ep - 1)], ids_recv_sem.at[0])
 
     loads[0].wait()
     ep_start(0)
     for h in (0, 1):
         line_start(tok_copy, h)
 
+    for load in loads[8:11]:
+        load.wait()
     for s in range(n_exp):
         row = chosen_ref[pl.ds(s, 1), :]
         col = column_of(row.astype(f32), cap).astype(i32)
@@ -486,8 +493,7 @@
     ep_level(2, ep_levels[0])
     for j in range(1, n_tp):
         disp_pass(j, 1)
-    for mask in ep_masks:
-        ids_wait(mask)
+    ids_wait()
     for k in range(n_exp):
         for e in range(n_ep):
             ids = ids_in[e, pl.ds(ret_slot(k), 1), :]
@@ -624,8 +630,7 @@
         acc[0] += in_down[tp].astype(f32)
 
     for k in range(n_exp):
-        for mask in ep_masks:
-            ret_wait(mask, k)
+        ret_wait(k)
         value = acc[0] + jnp.dot(
             picker[k], back[k].reshape(n_ep * slot_pad, width), preferred_element_type=f32
         )
@@ -634,42 +639,40 @@
         else:
             out_ref[...] = value.astype(bf16)
 
+    result = pltpu.make_async_copy(out_ref, out_hbm, local_sem.at[9])
+    result.start()
     for w in range(4):
-        for h in (0, 1):
-            for mask in range(n_ep):
-                for hop in later_hops(mask, orders[h]):
-                    ep_copy(w, h, mask, hop).wait_send()
-    for h in parts_of:
-        far_each(lambda copy: copy.wait_send(), h)
-    for up in (0, 1):
-        for j in range(n_tp - 1):
-
-            @pl.when(jnp.logical_and(known(up, j), ahead(up)))
-            def _():
-                for h in parts_of:
-                    tok_copy(up, j, h).wait_send()
-                    hid_copy(up, j, h).wait_send()
-
-        for j in range(n_tp):
-
-            @pl.when(jnp.logical_and(known(up, j), in_group(up)))
-            def _():
-                for h in parts_of:
-                    disp_copy(up, j, h).wait_send()
-
-    for mask in ep_masks:
-        ids_copy(mask).wait_send()
-        for k in range(n_exp):
-            ret_copy(mask, k).wait_send()
-    for d in range(n_tp):
-
-        @pl.when(tp < d)
-        def _():
-            up_copy(d).wait_send()
-
-        @pl.when(tp > d)
-        def _():
-            down_copy(d).wait_send()
+        if w == 0 or len(sg_in.shape) == 3:
+            sent = [tok_all, sg_in, su_in, sd_in][w].at[pl.ds(0, n_ep - 1)]
+        else:
+            cols = sg_hbm.shape[1] * (n_ep - 1)
+            sent = [None, sg_in, su_in, sd_in][w].at[:, pl.ds(0, cols)]
+        local_wait(sent, ep_send.at[w])
+    local_wait(sel.at[pl.ds(0, n_exp - 1)], far_send.at[0])
+    local_wait(ids_out.at[pl.ds(0, n_ep - 1)], ids_send_sem.at[0])
+    for k in range(n_exp):
+        local_wait(stage.at[k, pl.ds(0, n_ep - 1)], ret_send.at[k])
+    for place in range(n_tp):
+        for up in (0, 1):
+            blocks = place + 1 if up else n_tp - place
+            last = n_tp - 1 if up else 0
+            if place != last:
+
+                @pl.when(tp == place)
+                def _():
+                    local_wait(own_rows.at[:, pl.ds(0, blocks * width)], tp_send.at[up])
+                    local_wait(hidden.at[pl.ds(0, blocks)], hid_send.at[up])
+                    sums = up_send if up else down_send
+                    local_wait(parts.at[pl.ds(0, n_tp - blocks)], sums.at[0])
+
+            edge = place % split == (split - 1 if up else 0)
+            if not edge:
+
+                @pl.when(tp == place)
+                def _():
+                    local_wait(used_rows.at[:, pl.ds(0, blocks * width)], disp_send.at[up])
+
+    result.wait()
 
 
 def on_device(
@@ -700,15 +703,19 @@
     else:
         joined = (n_ep, rows, cols)
         flat = [pltpu.VMEM((rows, n_ep * cols), bf16)] * 3
-    vmem = pl.BlockSpec(memory_space=pltpu.VMEM)
-    hbm = pl.BlockSpec(memory_space=pl.ANY)
+    hbm = pl.BlockSpec(memory_space=pltpu.HBM)
+    anywhere = pl.BlockSpec(memory_space=pl.ANY)
     dma = pltpu.SemaphoreType.DMA
     return pl.pallas_call(
         functools.partial(layer_kernel, n_tp, n_ep, slot_most),
         out_shape=jax.ShapeDtypeStruct((n_tok, width), bf16),
-        in_specs=[hbm, vmem] + [hbm] * 6 + [vmem] * 2,
-        out_specs=vmem,
+        in_specs=[hbm] * 10,
+        out_specs=anywhere,
         scratch_shapes=[
+            pltpu.VMEM((n_tok, width), bf16),
+            pltpu.VMEM((1, model), f32),
+            pltpu.VMEM(chosen.shape, i32),
+            pltpu.VMEM(gates.shape, f32),
             pltpu.VMEM((n_ep, n_tok, width), bf16),
             pltpu.VMEM((n_tok, model), bf16),
             pltpu.VMEM((cap, model), bf16),
@@ -732,24 +739,24 @@
             pltpu.VMEM((n_exp, cap, 1), i32),
             pltpu.VMEM((n_exp, cap, 1), f32),
             pltpu.VMEM((n_exp, 1, cap), i32),
-            dma((4, 2, n_ep)),
-            dma((4, 2, n_ep)),
-            dma((2, n_tp, 2)),
-            dma((2, n_tp, 2)),
-            dma((2, n_tp, 2)),
+            dma((4,)),
+            dma((4, 2, n_ep - 1)),
+            dma((2,)),
+            dma((2, n_tp - 1, 2)),
+            dma((2,)),
             dma((n_tp, 2)),
-            dma((n_exp, 2)),
-            dma((2, n_tp, 2)),
-            dma((2, n_tp, 2)),
+            dma((1,)),
+            dma((2,)),
+            dma((2, n_tp - 1, 2)),
+            dma((1,)),
             dma((n_tp,)),
+            dma((1,)),
             dma((n_tp,)),
-            dma((n_tp,)),
-            dma((n_tp,)),
-            dma((n_ep, n_exp)),
-            dma((n_ep, n_exp)),
-            dma((n_ep,)),
-            dma((n_ep,)),
-            dma((9,)),
+            dma((n_exp,)),
+            dma((n_exp,)),
+            dma((1,)),
+            dma((1,)),
+            dma((13,)),
         ]
         + flat,
         compiler_params=pltpu.CompilerParams(

time: 109 us -> 107 us (0.982)
  Pallas kernels: 107 us -> 104 us
    pallas_call x1, Pallas kernels: 107 us -> 104 us  [on_device(): pl.pallas_call(functools.partial(layer_kernel, n_tp, n_ep, slot_most), ou...]
where the time goes in v4:
time: 107 us; the launch traced here: 106 us
  Pallas kernels  104 us (97%)
  local copies, waits for them, and re-layouts  1.77 us (2%)
    pallas_call x1, Pallas kernels, on_device(): pl.pallas_call(functools.partial(layer_kernel, n_tp, n_ep, slot_most), ou...  104 us

profile of v4, /device:TPU:0, one launch (start us, length us, event | category | flops | bytes accessed | tf_op | source)
XLA Modules:
  0.0 106.0 jit_solution(224814880603082247)
XLA Ops:
  0.0 104.3 %shard_map.100 = bf16[384,512]{1,0:T(8,128)(2,1)} custom-call(bf16[384,512]{1,0:T(8,128)(2,1)} %tok_hbm.1, f32[1,2048]{1,0:T(1,128)} %bitcast.11, bf16[704,256]{1,0:T(8,128)(2,1)} %bitcast.9, bf16[704,256]{1,0:T(8,128)(2,1)} %bitcast.10, bf16[704,256]{1,0:T(8,128)(2,1)} %sd_hbm.1, bf16[704,2048]{1,0:T(8,128)(2,1)} %bitcast.6, bf16[704,2048]{1,0:T(8,128)(2,1)} %bitcast.7, ...), custom_call_target="tpu_custom_call" | custom-call | tf_op jit(solution)/shard_map/pallas_call | solution.py:709
  104.3 1.8 %copy.12 = bf16[384,512]{1,0:T(8,128)(2,1)} copy(bf16[384,512]{1,0:T(8,128)(2,1)} %shard_map.100) | data formatting | bytes 786432

commit v5 on v4

--- a/solution.py
+++ b/solution.py
@@ -102,6 +102,10 @@
     chosen_col,
     gates_col,
     place_row,
+    place_col,
+    near_out,
+    near_in,
+    normed,
     ep_send,
     ep_recv,
     tp_send,
@@ -119,6 +123,8 @@
     ret_recv,
     ids_send_sem,
     ids_recv_sem,
+    near_send,
+    near_recv,
     local_sem,
     *flat,
 ):
@@ -135,6 +141,11 @@
     ep_levels = levels(n_ep)
     cut = max(128, cap * 2 // 3 // 128 * 128)
     chunks = [(0, cut), (cut, cap - cut)]
+    direct = n_tp == 4 and split == 2
+    at_end = jnp.logical_or(tp == 0, tp == n_tp - 1)
+    far_end = n_tp - 1 - tp
+    part = near_in.shape[2]
+    whole = direct and part == width
     parts_of = range(len(chunks))
 
     own_loads = [
@@ -278,9 +289,8 @@
                 def _():
                     copy(up, j, *rest).start()
 
-    def hid_pass(j, side):
-        for h in parts_of:
-            line_pass(hid_copy, hid_wait, j, h, side=side)
+    def hid_pass(j, side, h):
+        line_pass(hid_copy, hid_wait, j, h, side=side)
 
     def tok_pass(j, h):
         line_pass(tok_copy, tok_wait, j, h)
@@ -298,9 +308,15 @@
         cols = pl.ds(pl.multiple_of(block * width, width), width)
         return used_rows.at[pl.ds(*chunks[h]), cols]
 
+    def rest_piece(block, h):
+        cols = pl.ds(pl.multiple_of(block * width + part, 128), width - part)
+        return used_rows.at[pl.ds(*chunks[h]), cols]
+
     def disp_copy(up, j, h):
         block = at_distance(up, j)
         ref = used_piece(block, h)
+        if direct and j == n_tp - 2:
+            ref = rest_piece(block, h)
         source = sel.at[slot, pl.ds(*chunks[h]), :] if j == 0 else ref
         return remote(
             source,
@@ -314,6 +330,8 @@
     def disp_wait(up, j, h):
         block = at_distance(up, j)
         ref = used_piece(block, h)
+        if direct and j == n_tp - 1:
+            ref = rest_piece(block, h)
         remote(
             ref, ref, disp_send.at[up], disp_recv.at[block, h], "tp", at_distance(up, 1)
         ).wait_recv()
@@ -341,7 +359,6 @@
                 act(far_copy(k, h, s * split + split - 1))
 
     def disp_start(h):
-        far_each(lambda copy: copy.start(), h)
         for up in (0, 1):
 
             @pl.when(in_group(up))
@@ -354,29 +371,40 @@
             @pl.when(jnp.logical_and(known(up, j), in_group(up)))
             def _():
                 disp_wait(up, j, h)
-                disp_copy(up, j, h).start()
+                if not (whole and j == n_tp - 2):
+                    disp_copy(up, j, h).start()
 
     def disp_rest(h):
-        for j in range(1, n_tp):
+        for j in range(1, n_tp - 1 if whole else n_tp):
             for up in (0, 1):
 
                 @pl.when(jnp.logical_and(known(up, j), jnp.logical_not(in_group(up))))
                 def _():
                     disp_wait(up, j, h)
 
-    def up_copy(d):
-        return remote(parts.at[d], in_up.at[d], up_send.at[0], up_recv.at[d], "tp", tp + 1)
-
-    def down_copy(d):
-        return remote(parts.at[d], in_down.at[d], down_send.at[0], down_recv.at[d], "tp", tp - 1)
-
-    def up_wait(d):
-        ref = in_up.at[d]
-        remote(ref, ref, up_send.at[0], up_recv.at[d], "tp", tp - 1).wait_recv()
-
-    def down_wait(d):
-        ref = in_down.at[d]
-        remote(ref, ref, down_send.at[0], down_recv.at[d], "tp", tp + 1).wait_recv()
+    def sum_rows(h):
+        half = n_tok // 2
+        return pl.ds(pl.multiple_of(h * half, half), half)
+
+    def up_copy(d, h):
+        rows = (d, sum_rows(h))
+        return remote(
+            parts.at[rows], in_up.at[rows], up_send.at[0], up_recv.at[d, h], "tp", tp + 1
+        )
+
+    def down_copy(d, h):
+        rows = (d, sum_rows(h))
+        return remote(
+            parts.at[rows], in_down.at[rows], down_send.at[0], down_recv.at[d, h], "tp", tp - 1
+        )
+
+    def up_wait(d, h):
+        ref = in_up.at[d, sum_rows(h)]
+        remote(ref, ref, up_send.at[0], up_recv.at[d, h], "tp", tp - 1).wait_recv()
+
+    def down_wait(d, h):
+        ref = in_down.at[d, sum_rows(h)]
+        remote(ref, ref, down_send.at[0], down_recv.at[d, h], "tp", tp + 1).wait_recv()
 
     def ret_copy(mask, k):
         rows = pl.ds(0, slot_most)
@@ -394,6 +422,16 @@
 
     def ret_wait(k):
         local_wait(back.at[k, pl.ds(0, n_ep - 1), pl.ds(0, slot_most), :], ret_recv.at[k])
+
+    def near_copy(mask):
+        return remote(
+            near_out.at[flip(ep, mask)],
+            near_in.at[ep],
+            near_send.at[0],
+            near_recv.at[0],
+            "ep",
+            flip(ep, mask),
+        )
 
     def ids_copy(mask):
         return remote(
@@ -433,6 +471,7 @@
         rows = lax.broadcasted_iota(i32, (cap, 1), 0)
         place_row[s] = row_from * slot_most + lanes - run_row
         within = rows - run_col
+        place_col[s] = col_from * slot_most + within
 
         def slot_ids(d, carry):
             slots = lax.broadcasted_iota(i32, (cap, slot_pad), 1)
@@ -453,18 +492,32 @@
 
         lax.fori_loop(0, n_exp, one, 0)
 
-    select(ep)
-    if n_tp > 2:
-        tok_pass(1, 0)
-    ep_level(0, ep_levels[0])
-    for load in loads[1:4]:
-        load.wait()
-    for w in (1, 2, 3):
-        ep_start(w)
     ep_masks = sorted(range(1, n_ep), key=lambda m: -bin(m >> 1).count("1"))
     for mask in ep_masks:
         ids_copy(mask).start()
     ids_in[ep] = ids_out[ep]
+    select(ep)
+    if n_tp > 2:
+        tok_pass(1, 0)
+    def pick(k):
+        for e in range(n_ep):
+            ids = ids_in[e, pl.ds(ret_slot(k), 1), :]
+            match = lax.broadcasted_iota(i32, (n_tok, slot_pad), 0) == ids
+            picker[k, :, e * slot_pad : (e + 1) * slot_pad] = jnp.where(match, 1.0, 0.0).astype(bf16)
+
+    ids_wait()
+    pick(0)
+    ep_level(0, ep_levels[0])
+    for load in loads[1:4]:
+        load.wait()
+    ep_start(1)
+    held = at_end if direct else tp < 0
+
+    @pl.when(jnp.logical_not(held))
+    def _():
+        ep_start(2)
+        ep_start(3)
+
     if n_tp > 2:
         tok_pass(1, 1)
     for mask in ep_levels[0]:
@@ -477,29 +530,70 @@
             select(flip(ep, mask))
     for s in range(n_exp):
         sel[s] = acc[s].astype(bf16)
-    disp_start(0)
+    if n_tp > 3:
+        tok_pass(2, 1)
+    far_each(lambda copy: copy.start(), 0)
     own_used = pltpu.make_async_copy(sel.at[slot], columns(used_rows, tp), local_sem.at[8])
     own_used.start()
     acc[...] = jnp.zeros_like(acc)
-    if n_tp > 3:
-        tok_pass(2, 1)
     for j in range(3, n_tp - 1):
         for h in (0, 1):
             tok_pass(j, h)
     ep_level(1, ep_levels[0])
-    disp_start(1)
+
+    @pl.when(held)
+    def _():
+        ep_start(2)
+
+    far_each(lambda copy: copy.start(), 1)
+    for h in parts_of:
+        disp_start(h)
     for j in range(1, n_tp):
         disp_pass(j, 0)
+    if direct:
+
+        @pl.when(at_end)
+        def _():
+            for h in (0, 1):
+                tok_pass(n_tp - 1, h)
+            cols = pl.ds(pl.multiple_of(far_end * width, width), part)
+            rows = lax.dot_general(
+                picker[0], own_rows[:, cols], (((0,), (0,)), ((), ())), preferred_element_type=f32
+            )
+            near_out[...] = rows.reshape(n_ep, slot_pad, part)[:, :slot_most, :].astype(bf16)
+            for mask in ep_masks:
+                near_copy(mask).start()
+            near_in[ep] = near_out[ep]
+
+
+    @pl.when(held)
+    def _():
+        ep_start(3)
+
     ep_level(2, ep_levels[0])
     for j in range(1, n_tp):
         disp_pass(j, 1)
-    ids_wait()
-    for k in range(n_exp):
-        for e in range(n_ep):
-            ids = ids_in[e, pl.ds(ret_slot(k), 1), :]
-            match = lax.broadcasted_iota(i32, (n_tok, slot_pad), 0) == ids
-            picker[k, :, e * slot_pad : (e + 1) * slot_pad] = jnp.where(match, 1.0, 0.0).astype(bf16)
-    ep_level(3, ep_levels[0])
+    for k in range(1, n_exp):
+        pick(k)
+    @pl.when(jnp.logical_not(held))
+    def _():
+        ep_level(3, ep_levels[0])
+
+    if direct:
+
+        @pl.when(at_end)
+        def _():
+            local_wait(near_in.at[pl.ds(0, n_ep - 1)], near_recv.at[0])
+            slots = n_ep * slot_most
+            match = lax.broadcasted_iota(i32, (cap, slots), 1) == place_col[slot]
+            rows = jnp.dot(
+                jnp.where(match, 1.0, 0.0).astype(bf16),
+                near_in[...].reshape(slots, part),
+                preferred_element_type=f32,
+            )
+            cols = pl.ds(pl.multiple_of(far_end * width, width), part)
+            used_rows[:, cols] = rows.astype(bf16)
+
     own_used.wait()
     loads[5].wait()
     loads[6].wait()
@@ -511,12 +605,23 @@
         up = lax.dot_general(eu_ref[...], used, contract, preferred_element_type=f32)
         hidden[tp, :, pl.ds(*chunks[h])] = (jax.nn.silu(gate) * up).astype(bf16)
         line_start(hid_copy, h)
+    loads[4].wait()
+    if not direct:
+        for h in (0, 1):
+            tok_pass(n_tp - 1, h)
+    def norm_rows(i, carry):
+        rows = sum_rows(i)
+        normed[rows, :] = normalise(own_rows[rows, :], gain_ref[...])
+        return carry
+
+    lax.fori_loop(0, 2, norm_rows, 0)
+    @pl.when(held)
+    def _():
+        ep_level(3, ep_levels[0])
+
     for masks in ep_levels[1:]:
         for w in (1, 2, 3):
             ep_level(w, masks)
-    loads[4].wait()
-    for h in (0, 1):
-        tok_pass(n_tp - 1, h)
     if flat:
         weights = flat
         cols = sg_hbm.shape[1]
@@ -530,9 +635,19 @@
     sg_ref, su_ref, sd_ref = weights
     chunk = n_tok // 2
 
+    def sums_first(h):
+        @pl.when(tp == 0)
+        def _():
+            up_copy(n_tp - 1, h).start()
+
+        @pl.when(tp == n_tp - 1)
+        def _():
+            down_copy(0, h).start()
+
+
     def shared_rows(i, carry):
         rows = pl.ds(pl.multiple_of(i * chunk, chunk), chunk)
-        x = normalise(own_rows[rows, :], gain_ref[...])
+        x = normed[rows, :]
         contract = (((1,), (1,)), ((), ()))
         gate = lax.dot_general(x, sg_ref[...], contract, preferred_element_type=f32)
         up = lax.dot_general(x, su_ref[...], contract, preferred_element_type=f32)
@@ -542,6 +657,7 @@
             parts[block, rows, :] = jnp.dot(
                 mid, sd_ref[:, cols], preferred_element_type=f32
             ).astype(bf16)
+        sums_first(i)
         return carry
 
     lax.fori_loop(0, 2, shared_rows, 0)
@@ -549,43 +665,60 @@
     def sums_ends(j):
         @pl.when(tp == 0)
         def _():
-            up_copy(n_tp - 1 - j).start()
+            for h in (0, 1):
+                up_copy(n_tp - 1 - j, h).start()
 
         @pl.when(tp == n_tp - 1)
         def _():
-            down_copy(j).start()
+            for h in (0, 1):
+                down_copy(j, h).start()
 
     def sums_up(j):
         d = n_tp - 1 - j
 
         @pl.when(jnp.logical_and(tp > 0, tp < d))
         def _():
-            up_wait(d)
-            parts[d] = (parts[d].astype(f32) + in_up[d].astype(f32)).astype(bf16)
-            up_copy(d).start()
+            for h in (0, 1):
+                rows = sum_rows(h)
+                up_wait(d, h)
+                parts[d, rows] = (parts[d, rows].astype(f32) + in_up[d, rows].astype(f32)).astype(bf16)
+                up_copy(d, h).start()
 
     def sums_down(j):
         @pl.when(jnp.logical_and(tp < n_tp - 1, tp > j))
         def _():
-            down_wait(j)
-            parts[j] = (parts[j].astype(f32) + in_down[j].astype(f32)).astype(bf16)
-            down_copy(j).start()
-
-    def sums_middle(j):
+            for h in (0, 1):
+                rows = sum_rows(h)
+                down_wait(j, h)
+                parts[j, rows] = (parts[j, rows].astype(f32) + in_down[j, rows].astype(f32)).astype(bf16)
+                down_copy(j, h).start()
+
+    def sums_outer(j):
         @pl.when(tp < n_tp // 2)
         def _():
             sums_up(j)
+
+        @pl.when(tp >= n_tp // 2)
+        def _():
             sums_down(j)
 
+    def sums_inner(j):
+        @pl.when(tp < n_tp // 2)
+        def _():
+            sums_down(j)
+
         @pl.when(tp >= n_tp // 2)
         def _():
-            sums_down(j)
             sums_up(j)
 
-    def add_block(mask):
+    def add_block(mask, h):
         block = flip(tp, mask)
-        acc[block // split] += lax.dot_general(
-            hidden[block], down_ref[block], (((0,), (0,)), ((), ())), preferred_element_type=f32
+        rows = pl.ds(*chunks[h])
+        acc[block // split, rows, :] += lax.dot_general(
+            hidden[block, :, rows],
+            down_ref[block],
+            (((0,), (0,)), ((), ())),
+            preferred_element_type=f32,
         )
 
     def give_back(k):
@@ -601,46 +734,62 @@
         back[k, ep, :slot_most, :] = stage[k, ep]
 
     loads[7].wait()
-    sums_ends(0)
-    add_block(0)
-    hid_pass(1, 0)
-    hid_pass(1, 1)
+    for h in parts_of:
+        add_block(0, h)
+    for h in parts_of:
+        hid_pass(1, 0, h)
+    for h in parts_of:
+        hid_pass(1, 1, h)
     for j in range(1, n_tp):
         if j > 1:
-            hid_pass(j, 0)
-            hid_pass(j, 1)
-        add_block(j)
+            for h in parts_of:
+                hid_pass(j, 0, h)
+                hid_pass(j, 1, h)
+                add_block(j, h)
+        if j == 1:
+            for h in parts_of:
+                add_block(j, h)
         if (j + 1) % split == 0:
             give_back(j // split)
         if j > 1:
-            sums_middle(j - 2)
+            sums_outer(j - 2)
         if j < n_tp - 1:
             sums_ends(j)
-    sums_middle(n_tp - 2)
+    sums_outer(n_tp - 2)
+    for j in range(n_tp - 1):
+        sums_inner(j)
     acc[0] = parts[tp].astype(f32)
 
     @pl.when(tp > 0)
     def _():
-        up_wait(tp)
+        for h in (0, 1):
+            up_wait(tp, h)
         acc[0] += in_up[tp].astype(f32)
 
     @pl.when(tp < n_tp - 1)
     def _():
-        down_wait(tp)
+        for h in (0, 1):
+            down_wait(tp, h)
         acc[0] += in_down[tp].astype(f32)
 
     for k in range(n_exp):
         ret_wait(k)
-        value = acc[0] + jnp.dot(
-            picker[k], back[k].reshape(n_ep * slot_pad, width), preferred_element_type=f32
-        )
-        if k < n_exp - 1:
-            acc[0] = value
-        else:
-            out_ref[...] = value.astype(bf16)
-
-    result = pltpu.make_async_copy(out_ref, out_hbm, local_sem.at[9])
-    result.start()
+        for h in (0, 1):
+            rows = sum_rows(h)
+            value = acc[0, rows, :] + jnp.dot(
+                picker[k, rows, :],
+                back[k].reshape(n_ep * slot_pad, width),
+                preferred_element_type=f32,
+            )
+            if k < n_exp - 1:
+                acc[0, rows, :] = value
+            else:
+                out_ref[rows, :] = value.astype(bf16)
+                result = pltpu.make_async_copy(
+                    out_ref.at[rows, :], out_hbm.at[rows, :], local_sem.at[8 + h]
+                )
+                result.start()
+
     for w in range(4):
         if w == 0 or len(sg_in.shape) == 3:
             sent = [tok_all, sg_in, su_in, sd_in][w].at[pl.ds(0, n_ep - 1)]
@@ -649,6 +798,12 @@
             sent = [None, sg_in, su_in, sd_in][w].at[:, pl.ds(0, cols)]
         local_wait(sent, ep_send.at[w])
     local_wait(sel.at[pl.ds(0, n_exp - 1)], far_send.at[0])
+    if direct:
+
+        @pl.when(at_end)
+        def _():
+            local_wait(near_out.at[pl.ds(0, n_ep - 1)], near_send.at[0])
+
     local_wait(ids_out.at[pl.ds(0, n_ep - 1)], ids_send_sem.at[0])
     for k in range(n_exp):
         local_wait(stage.at[k, pl.ds(0, n_ep - 1)], ret_send.at[k])
@@ -670,9 +825,16 @@
 
                 @pl.when(tp == place)
                 def _():
-                    local_wait(used_rows.at[:, pl.ds(0, blocks * width)], disp_send.at[up])
-
-    result.wait()
+                    sent = blocks * width
+                    if direct and place == (n_tp - 2 if up else 1):
+                        sent = sent - part
+                    local_wait(used_rows.at[:, pl.ds(0, sent)], disp_send.at[up])
+
+    for h in (0, 1):
+        rows = sum_rows(h)
+        pltpu.make_async_copy(
+            out_ref.at[rows, :], out_hbm.at[rows, :], local_sem.at[8 + h]
+        ).wait()
 
 
 def on_device(
@@ -696,6 +858,7 @@
     slot_most = 2 * cap // n_ep
     slot_pad = -(-slot_most // 128) * 128
     n_hid = expert_gate.shape[2]
+    near = width
     sg, su, sd = shared_gate.T, shared_up.T, shared_down
     rows, cols = sg.shape
     if cols % 128 == 0:
@@ -739,6 +902,10 @@
             pltpu.VMEM((n_exp, cap, 1), i32),
             pltpu.VMEM((n_exp, cap, 1), f32),
             pltpu.VMEM((n_exp, 1, cap), i32),
+            pltpu.VMEM((n_exp, cap, 1), i32),
+            pltpu.VMEM((n_ep, slot_most, near), bf16),
+            pltpu.VMEM((n_ep, slot_most, near), bf16),
+            pltpu.VMEM((n_tok, model), bf16),
             dma((4,)),
             dma((4, 2, n_ep - 1)),
             dma((2,)),
@@ -749,11 +916,13 @@
             dma((2,)),
             dma((2, n_tp - 1, 2)),
             dma((1,)),
-            dma((n_tp,)),
+            dma((n_tp, 2)),
             dma((1,)),
-            dma((n_tp,)),
+            dma((n_tp, 2)),
             dma((n_exp,)),
             dma((n_exp,)),
+            dma((1,)),
+            dma((1,)),
             dma((1,)),
             dma((1,)),
             dma((13,)),

time: 107 us -> 105 us (0.981)
  Pallas kernels: 104 us -> 102 us
    pallas_call x1, Pallas kernels: 104 us -> 102 us  [on_device(): pl.pallas_call(functools.partial(layer_kernel, n_tp, n_ep, slot_most), ou...]
where the time goes in v5:
time: 105 us; the launch traced here: 104 us
  Pallas kernels  102 us (97%)
  local copies, waits for them, and re-layouts  1.77 us (2%)
    pallas_call x1, Pallas kernels, on_device(): pl.pallas_call(functools.partial(layer_kernel, n_tp, n_ep, slot_most), ou...  102 us

profile of v5, /device:TPU:0, one launch (start us, length us, event | category | flops | bytes accessed | tf_op | source)
XLA Modules:
  0.0 104.2 jit_solution(10859222131063806606)
XLA Ops:
  0.0 102.4 %shard_map.100 = bf16[384,512]{1,0:T(8,128)(2,1)} custom-call(bf16[384,512]{1,0:T(8,128)(2,1)} %tok_hbm.1, f32[1,2048]{1,0:T(1,128)} %bitcast.11, bf16[704,256]{1,0:T(8,128)(2,1)} %bitcast.9, bf16[704,256]{1,0:T(8,128)(2,1)} %bitcast.10, bf16[704,256]{1,0:T(8,128)(2,1)} %sd_hbm.1, bf16[704,2048]{1,0:T(8,128)(2,1)} %bitcast.6, bf16[704,2048]{1,0:T(8,128)(2,1)} %bitcast.7, ...), custom_call_target="tpu_custom_call" | custom-call | tf_op jit(solution)/shard_map/pallas_call | solution.py:872
  102.4 1.8 %copy.12 = bf16[384,512]{1,0:T(8,128)(2,1)} copy(bf16[384,512]{1,0:T(8,128)(2,1)} %shard_map.100) | data formatting | bytes 786432

commit v6 on v5

--- a/solution.py
+++ b/solution.py
@@ -106,6 +106,7 @@
     near_out,
     near_in,
     normed,
+    mid_ref,
     ep_send,
     ep_recv,
     tp_send,
@@ -513,9 +514,10 @@
     ep_start(1)
     held = at_end if direct else tp < 0
 
+    ep_start(2)
+
     @pl.when(jnp.logical_not(held))
     def _():
-        ep_start(2)
         ep_start(3)
 
     if n_tp > 2:
@@ -541,10 +543,6 @@
             tok_pass(j, h)
     ep_level(1, ep_levels[0])
 
-    @pl.when(held)
-    def _():
-        ep_start(2)
-
     far_each(lambda copy: copy.start(), 1)
     for h in parts_of:
         disp_start(h)
@@ -620,38 +618,47 @@
         ep_level(3, ep_levels[0])
 
     for masks in ep_levels[1:]:
-        for w in (1, 2, 3):
+        for w in (1, 2):
             ep_level(w, masks)
-    if flat:
-        weights = flat
-        cols = sg_hbm.shape[1]
-        group = 128 // cols
-        for ref, out in zip((sg_in, su_in, sd_in), flat):
-            for j in range(n_ep // group):
-                joined = jnp.concatenate([ref[j * group + i] for i in range(group)], axis=1)
-                out[:, j * 128 : (j + 1) * 128] = joined
-    else:
-        weights = (sg_in, su_in, sd_in)
-    sg_ref, su_ref, sd_ref = weights
-    chunk = n_tok // 2
-
-    def sums_first(h):
-        @pl.when(tp == 0)
-        def _():
-            up_copy(n_tp - 1, h).start()
-
-        @pl.when(tp == n_tp - 1)
-        def _():
-            down_copy(0, h).start()
-
-
-    def shared_rows(i, carry):
-        rows = pl.ds(pl.multiple_of(i * chunk, chunk), chunk)
+    def join(k):
+        if not flat:
+            return (sg_in, su_in, sd_in)[k]
+        group = 128 // sg_hbm.shape[1]
+        blocks, out = (sg_in, su_in, sd_in)[k], flat[k]
+        for j in range(n_ep // group):
+            joined = jnp.concatenate([blocks[j * group + i] for i in range(group)], axis=1)
+            out[:, j * 128 : (j + 1) * 128] = joined
+        return out
+
+    sg_ref, su_ref = join(0), join(1)
+
+    def shared_up(i, carry):
+        rows = sum_rows(i)
         x = normed[rows, :]
         contract = (((1,), (1,)), ((), ()))
         gate = lax.dot_general(x, sg_ref[...], contract, preferred_element_type=f32)
         up = lax.dot_general(x, su_ref[...], contract, preferred_element_type=f32)
-        mid = (jax.nn.silu(gate) * up).astype(bf16)
+        mid_ref[rows, :] = (jax.nn.silu(gate) * up).astype(bf16)
+        return carry
+
+    lax.fori_loop(0, 2, shared_up, 0)
+    for masks in ep_levels[1:]:
+        ep_level(3, masks)
+    sd_ref = join(2)
+
+    def sums_first(h):
+        @pl.when(tp == 0)
+        def _():
+            up_copy(n_tp - 1, h).start()
+
+        @pl.when(tp == n_tp - 1)
+        def _():
+            down_copy(0, h).start()
+
+
+    def shared_rows(i, carry):
+        rows = sum_rows(i)
+        mid = mid_ref[rows, :]
         for block in range(n_tp):
             cols = pl.ds(block * width, width)
             parts[block, rows, :] = jnp.dot(
@@ -906,6 +913,7 @@
             pltpu.VMEM((n_ep, slot_most, near), bf16),
             pltpu.VMEM((n_ep, slot_most, near), bf16),
             pltpu.VMEM((n_tok, model), bf16),
+            pltpu.VMEM((n_tok, rows), bf16),
             dma((4,)),
             dma((4, 2, n_ep - 1)),
             dma((2,)),

time: 105 us -> 102 us (0.971)
  Pallas kernels: 102 us -> 100 us
    pallas_call x1, Pallas kernels: 102 us -> 100 us  [on_device(): pl.pallas_call(functools.partial(layer_kernel, n_tp, n_ep, slot_most), ou...]
where the time goes in v6:
time: 102 us
  Pallas kernels  100 us (98%)
  local copies, waits for them, and re-layouts  1.77 us (2%)
    pallas_call x1, Pallas kernels, on_device(): pl.pallas_call(functools.partial(layer_kernel, n_tp, n_ep, slot_most), ou...  100 us

profile of v6, /device:TPU:0, one launch (start us, length us, event | category | flops | bytes accessed | tf_op | source)
XLA Modules:
  0.0 101.9 jit_solution(1587348258235901003)
XLA Ops:
  0.0 100.1 %shard_map.100 = bf16[384,512]{1,0:T(8,128)(2,1)} custom-call(bf16[384,512]{1,0:T(8,128)(2,1)} %tok_hbm.1, f32[1,2048]{1,0:T(1,128)} %bitcast.11, bf16[704,256]{1,0:T(8,128)(2,1)} %bitcast.9, bf16[704,256]{1,0:T(8,128)(2,1)} %bitcast.10, bf16[704,256]{1,0:T(8,128)(2,1)} %sd_hbm.1, bf16[704,2048]{1,0:T(8,128)(2,1)} %bitcast.6, bf16[704,2048]{1,0:T(8,128)(2,1)} %bitcast.7, ...), custom_call_target="tpu_custom_call" | custom-call | tf_op jit(solution)/shard_map/pallas_call | solution.py:879
  100.1 1.8 %copy.12 = bf16[384,512]{1,0:T(8,128)(2,1)} copy(bf16[384,512]{1,0:T(8,128)(2,1)} %shard_map.100) | data formatting | bytes 786432

commit v7 on v6

--- a/solution.py
+++ b/solution.py
@@ -680,43 +680,41 @@
             for h in (0, 1):
                 down_copy(j, h).start()
 
-    def sums_up(j):
+    def sums_up(j, h):
         d = n_tp - 1 - j
 
         @pl.when(jnp.logical_and(tp > 0, tp < d))
         def _():
-            for h in (0, 1):
-                rows = sum_rows(h)
-                up_wait(d, h)
-                parts[d, rows] = (parts[d, rows].astype(f32) + in_up[d, rows].astype(f32)).astype(bf16)
-                up_copy(d, h).start()
-
-    def sums_down(j):
+            rows = sum_rows(h)
+            up_wait(d, h)
+            parts[d, rows] = (parts[d, rows].astype(f32) + in_up[d, rows].astype(f32)).astype(bf16)
+            up_copy(d, h).start()
+
+    def sums_down(j, h):
         @pl.when(jnp.logical_and(tp < n_tp - 1, tp > j))
         def _():
-            for h in (0, 1):
-                rows = sum_rows(h)
-                down_wait(j, h)
-                parts[j, rows] = (parts[j, rows].astype(f32) + in_down[j, rows].astype(f32)).astype(bf16)
-                down_copy(j, h).start()
-
-    def sums_outer(j):
+            rows = sum_rows(h)
+            down_wait(j, h)
+            parts[j, rows] = (parts[j, rows].astype(f32) + in_down[j, rows].astype(f32)).astype(bf16)
+            down_copy(j, h).start()
+
+    def sums_outer(j, h):
         @pl.when(tp < n_tp // 2)
         def _():
-            sums_up(j)
+            sums_up(j, h)
 
         @pl.when(tp >= n_tp // 2)
         def _():
-            sums_down(j)
-
-    def sums_inner(j):
+            sums_down(j, h)
+
+    def sums_inner(j, h):
         @pl.when(tp < n_tp // 2)
         def _():
-            sums_down(j)
+            sums_down(j, h)
 
         @pl.when(tp >= n_tp // 2)
         def _():
-            sums_up(j)
+            sums_up(j, h)
 
     def add_block(mask, h):
         block = flip(tp, mask)
@@ -759,12 +757,17 @@
         if (j + 1) % split == 0:
             give_back(j // split)
         if j > 1:
-            sums_outer(j - 2)
+            for h in (0, 1):
+                sums_outer(j - 2, h)
+                if j > 2:
+                    sums_inner(j - 3, h)
         if j < n_tp - 1:
             sums_ends(j)
-    sums_outer(n_tp - 2)
-    for j in range(n_tp - 1):
-        sums_inner(j)
+    for j in (n_tp - 3, n_tp - 2):
+        for h in (0, 1):
+            if j == n_tp - 2:
+                sums_outer(j, h)
+            sums_inner(j, h)
     acc[0] = parts[tp].astype(f32)
 
     @pl.when(tp > 0)

time: 102 us -> 102 us (level)
  no operation moved by 1% of the time
where the time goes in v7:
time: 102 us
  Pallas kernels  100 us (98%)
  local copies, waits for them, and re-layouts  1.77 us (2%)
    pallas_call x1, Pallas kernels, on_device(): pl.pallas_call(functools.partial(layer_kernel, n_tp, n_ep, slot_most), ou...  100 us

profile of v7, /device:TPU:0, one launch (start us, length us, event | category | flops | bytes accessed | tf_op | source)
XLA Modules:
  0.0 101.9 jit_solution(199897985488828539)
XLA Ops:
  0.0 100.1 %shard_map.100 = bf16[384,512]{1,0:T(8,128)(2,1)} custom-call(bf16[384,512]{1,0:T(8,128)(2,1)} %tok_hbm.1, f32[1,2048]{1,0:T(1,128)} %bitcast.11, bf16[704,256]{1,0:T(8,128)(2,1)} %bitcast.9, bf16[704,256]{1,0:T(8,128)(2,1)} %bitcast.10, bf16[704,256]{1,0:T(8,128)(2,1)} %sd_hbm.1, bf16[704,2048]{1,0:T(8,128)(2,1)} %bitcast.6, bf16[704,2048]{1,0:T(8,128)(2,1)} %bitcast.7, ...), custom_call_target="tpu_custom_call" | custom-call | tf_op jit(solution)/shard_map/pallas_call | solution.py:882
  100.1 1.8 %copy.12 = bf16[384,512]{1,0:T(8,128)(2,1)} copy(bf16[384,512]{1,0:T(8,128)(2,1)} %shard_map.100) | data formatting | bytes 786432
